TPU v7x, 256 devices: a whole 4x4x8 slice. The times are simulated.
256 devices in a mesh: leaf: 64 (over y, z, core), grid: 4 (over x).
Axes of the slice: x: 4, y: 4, z: 8, core: 2. Of those that a mesh axis runs over, the one named last changes fastest.
Arguments:
- source_leaf: float32 [8, 32768], P(None, ('leaf', 'grid')), may hold values from -6 to 6
- block_leaf: float32 [32768, 128], P(('leaf', 'grid')), may hold values from -0.5 to 0.5
- expand_leaf: float32 [32768, 128], P(('leaf', 'grid')), may hold values from -0.5 to 0.5
- basis_leaf: float32 [32768, 256], P(('leaf', 'grid')), may hold values from -0.25 to 0.25
- pivot_leaf: float32 [32768], P(('leaf', 'grid')), may hold values from -2 to 2
- couple_leaf: float32 [65536, 128], P(('leaf', 'grid')), may hold values from -0.5 to 0.5
- ranks_leaf: int32 [64, 2], replicated, may hold values from 32 to 128
- targets_leaf: int32 [65536], P(('leaf', 'grid')), may hold values from 0 to 16383, as said below
- source_middle: float32 [8, 32768], P(None, ('leaf', 'grid')), may hold values from -6 to 6
- block_middle: float32 [32768, 128], P(('leaf', 'grid')), may hold values from -0.5 to 0.5
- expand_middle: float32 [32768, 128], P(('leaf', 'grid')), may hold values from -0.5 to 0.5
- basis_middle: float32 [32768, 256], P(('leaf', 'grid')), may hold values from -0.0625 to 0.0625
- pivot_middle: float32 [32768], P(('leaf', 'grid')), may hold values from -2 to 2
- couple_middle: float32 [32768, 128], P(('leaf', 'grid')), may hold values from -0.5 to 0.5
- ranks_middle: int32 [4, 2], replicated, may hold values from 32 to 128
- targets_middle: int32 [32768], P(('leaf', 'grid')), may hold values from 0 to 32767, as said below
- source_upper: float32 [8, 32768], P(None, ('leaf', 'grid')), may hold values from -6 to 6
- block_upper: float32 [32768, 128], P(('leaf', 'grid')), may hold values from -0.5 to 0.5
- expand_upper: float32 [32768, 128], P(('leaf', 'grid')), may hold values from -0.5 to 0.5
- basis_upper: float32 [32768, 256], P(('leaf', 'grid')), may hold values from -0.046875 to 0.046875
- pivot_upper: float32 [32768], P(('leaf', 'grid')), may hold values from -2 to 2
- couple_upper: float32 [32768, 128], P(('leaf', 'grid')), may hold values from -0.5 to 0.5
- ranks_upper: int32 [2, 2], replicated, may hold values from 32 to 128
- targets_upper: int32 [32768], P(('leaf', 'grid')), may hold values from 0 to 32767, as said below
- source_root: float32 [8, 32768], P(None, ('leaf', 'grid')), may hold values from -6 to 6
- block_root: float32 [32768, 128], P(('leaf', 'grid')), may hold values from -0.5 to 0.5
- expand_root: float32 [32768, 128], P(('leaf', 'grid')), may hold values from -0.5 to 0.5
- basis_root: float32 [32768, 256], P(('leaf', 'grid')), may hold values from -0.03125 to 0.03125
- pivot_root: float32 [32768], P(('leaf', 'grid')), may hold values from -2 to 2
- ranks_root: int32 [1, 2], replicated, may hold values from 32 to 128
Outputs:
- answer_leaf: float32 [8, 32768], P(None, ('leaf', 'grid'))
- answer_middle: float32 [8, 32768], P(None, ('leaf', 'grid'))
- answer_upper: float32 [8, 32768], P(None, ('leaf', 'grid'))
- answer_root: float32 [8, 32768], P(None, ('leaf', 'grid'))
Inputs may be any that keep to these rules, and one draw needn't show every extreme that they name: `targets_leaf`: within one leaf front the 1024 entries are distinct; each names a row of the parent front's row vector of 16384 rows. Split that vector's separator part and its update part each evenly, in order, over the parent's devices (leaf then grid); then the rows of one device name at most 4 rows held by any one of them, and exactly that many for some. `targets_middle`: within one middle front the entries are distinct; each names a row of the parent front's row vector of 32768 rows. Split likewise over the parent's devices, the rows of one device name at most 1 row held by any one of them, and exactly that many for some. `targets_upper`: within one upper front the entries are distinct; each names a row of the root separator. Split evenly in order over all devices, the rows of one device name at most 1 row held by any one of them, and exactly that many for some.
All inputs are finite; a program needn't handle non-finite values.
Results may differ from a plain program's by a relative error of at most 0.0003.
Values sent between devices are 32-bit elements; how exact they have to be, the bound alone decides.
No kernel may reach another device: no remote copies, remote signals or barrier semaphores. Data moves between devices by JAX's collectives and lax.ppermute only.
A program may use at most 128 MiB of HBM per device.

v0:
```python
import functools

import jax
import jax.numpy as jnp
from jax import lax
from jax.experimental import pallas as pl
from jax.experimental.pallas import tpu as pltpu
from jax.sharding import PartitionSpec as P


RHS = 8
LANES = 128
TILE = 128
HOLD = 8
SLOT = 16
SLOTS_LEAF = 4

SRC, WAT, QAT, VAT, MISC, CAT, PAT, END = 0, 8, 136, 264, 392, 400, 528, 656
RMISC, RPAT, REND = 264, 272, 400

F32 = jnp.float32
BF16 = jnp.bfloat16


def iota(shape, dim):
    return lax.broadcasted_iota(jnp.int32, shape, dim)


def raw(a, b, ca, cb):
    return lax.dot_general(a, b, (((ca,), (cb,)), ((), ())), preferred_element_type=F32)


def halves(a):
    high = a.astype(BF16)
    low = (a - high.astype(F32)).astype(BF16)
    return high, low


def stacked(a):
    high = a.astype(BF16).astype(F32)
    return jnp.concatenate([high, a - high], axis=0).astype(BF16)


def fold(total):
    rows = total.shape[0] // 2
    return total[0:rows] + total[rows:]


def dot(a, b, ca, cb):
    high, low = halves(b)
    both = stacked(a)
    return fold(raw(both, high, ca, cb) + raw(both, low, ca, cb))


def mm(a, b):
    return dot(a, b, 1, 0)


def mmt(a, b):
    return dot(a, b, 1, 1)


def cross(a, b):
    a_high, a_low = halves(a)
    b_high, b_low = halves(b)
    return (raw(a_low, b_high, 0, 0) + raw(a_high, b_low, 0, 0)) + raw(a_high, b_high, 0, 0)


def mask_rows(ranks_ref, groups, fronts_dim):
    front = lax.axis_index("leaf") // groups
    both = ranks_ref[...].astype(F32)
    own = iota(both.shape, fronts_dim) == front
    pair = jnp.sum(jnp.where(own, both, 0.0), axis=fronts_dim, keepdims=True)
    lane = iota((1, TILE), 1).astype(F32)
    if fronts_dim == 0:
        return [(lane < pair[:, i : i + 1]).astype(F32) for i in range(2)]
    return [(lane < pair[i : i + 1, :]).astype(F32) for i in range(2)]


def masks(rows_ref, level):
    return rows_ref[2 * level : 2 * level + 1, :], rows_ref[2 * level + 1 : 2 * level + 2, :]


def split_target(targets, shift):
    piece = lax.shift_right_logical(targets, shift)
    within = jnp.bitwise_and(targets, (1 << shift) - 1)
    dest = lax.shift_right_logical(within, 7)
    label = piece * TILE + jnp.bitwise_and(within, TILE - 1)
    return dest, label.astype(F32)


def row_onehot(at, count):
    n = at.shape[1]
    if at.dtype == jnp.int32:
        rows = iota((count, n), 0)
    else:
        rows = iota((count, n), 0).astype(F32)
    return (rows == jnp.broadcast_to(at, (count, n))).astype(F32)


def leaf_slots(onehot):
    n = onehot.shape[1]
    upper = (iota((n, n), 0) <= iota((n, n), 1)).astype(BF16)
    order = raw(onehot.astype(BF16), upper, 1, 0)
    return jnp.sum(order * onehot, axis=0, keepdims=True) - 1.0


def label_rows(label):
    n = label.shape[1]
    return jnp.where(iota((SLOT - RHS, n), 0) == 0, jnp.broadcast_to(label, (SLOT - RHS, n)), 0.0)


def fill(rows, n):
    used = sum(r.shape[0] for r in rows)
    if used < LANES:
        rows = rows + [jnp.zeros((LANES - used, n), F32)]
    return jnp.concatenate(rows, axis=0)


def block_mask(n, half=None):
    if half is None:
        lane = jnp.bitwise_and(iota((RHS, n), 1), HOLD - 1)
    else:
        lane = jnp.bitwise_and(iota((RHS, n), 1), 3) + 4 * half
    return jnp.concatenate([(lane == at).astype(F32) for at in numbers()], axis=0)


def slot_masks(n, halves_of):
    if halves_of:
        return [block_mask(n, k // SLOTS_LEAF) for k in range(2 * SLOTS_LEAF)]
    return [block_mask(n)] * HOLD


def received(turned, halves_of, cols):
    total = None
    for k, mask in enumerate(slot_masks(turned.shape[1], halves_of)):
        values = turned[SLOT * k : SLOT * k + RHS, :]
        label = turned[SLOT * k + RHS : SLOT * k + RHS + 1, :]
        spread = jnp.concatenate([values] * HOLD, axis=0) * mask
        part = raw(stacked(spread), row_onehot(label, cols).astype(BF16), 1, 1)
        total = part if total is None else total + part
    return fold(total)


def replies(turned, halves_of, rows):
    n = turned.shape[1]
    both = stacked(rows)
    out = []
    for k, mask in enumerate(slot_masks(n, halves_of)):
        label = turned[SLOT * k + RHS : SLOT * k + RHS + 1, :]
        found = fold(raw(both, row_onehot(label, rows.shape[1]).astype(BF16), 1, 0)) * mask
        one = found[0:RHS]
        for j in range(1, HOLD):
            one = one + found[RHS * j : RHS * (j + 1)]
        out += [one, jnp.zeros((SLOT - RHS, n), F32)]
    return fill(out, n).T


def slot_rows(at):
    return pl.ds(pl.multiple_of(SLOT * at, SLOT), SLOT)


def messages(blocks, targets, shift, count, scratch):
    for r, at in enumerate(numbers()):
        dest, label = split_target(targets[r : r + 1], shift)
        one = jnp.concatenate([blocks[r], label_rows(label)], axis=0)
        found = fold(raw(stacked(one), row_onehot(dest, count).astype(BF16), 1, 1))
        scratch[slot_rows(at), :] = found
    return scratch[...].T


def fetched(back, targets, shift, scratch):
    scratch[...] = back.T
    count = scratch.shape[1]
    out = []
    for r, at in enumerate(numbers()):
        dest, _ = split_target(targets[r : r + 1], shift)
        values = scratch[slot_rows(at), :][0:RHS]
        out.append(fold(raw(stacked(values), row_onehot(dest, count).astype(BF16), 1, 0)))
    return out


def lanes(blocks):
    return jnp.concatenate(blocks, axis=1)


def tall(blocks):
    return jnp.concatenate(blocks, axis=0)


def cut_lanes(value):
    return [value[:, TILE * b : TILE * (b + 1)] for b in range(HOLD)]


def cut_tall(value):
    return [value[RHS * b : RHS * (b + 1)] for b in range(HOLD)]


def own_number():
    core = jnp.bitwise_and(lax.axis_index("leaf"), 1)
    return core * 4 + lax.axis_index("grid")


def numbers():
    core = jnp.bitwise_and(lax.axis_index("leaf"), 1)
    at = lax.axis_index("grid")
    out = []
    for c in (core, 1 - core):
        for step in (0, 3, 1, 2):
            out.append(c * 4 + jnp.bitwise_and(at + step, 3))
    return out


class Held:
    def __init__(self, refs, cut, base=0):
        own, prev, after, low, high = refs[0:5]
        self.own = (own, prev, after)
        self.opposite = (low, high)
        self.core = refs[5:8]
        self.core_opposite = refs[8:10]
        self.cut = cut
        self.base = base

    def one(self, b, at, rows=TILE):
        at = at + self.base
        singles, split = (
            (self.own, self.opposite) if b < 4 else (self.core, self.core_opposite)
        )
        if b % 4 < 3:
            ref = singles[b % 4]
        elif at < self.cut:
            ref = split[0]
        else:
            ref = split[1]
            at = at - self.cut
        return ref[at : at + rows, :]

    def all(self, at):
        return jnp.concatenate([self.one(b, at) for b in range(HOLD)], axis=0)

    def misc(self, at, row):
        return jnp.concatenate([self.one(b, at + row, 1) for b in range(HOLD)], axis=0)


class Fetched(Held):
    def __init__(self, refs, cut, low, high, scratch, sems):
        self.low = low
        self.scratch = scratch
        self.copies = []
        own, core = refs[0:5], refs[5:10]
        for half, bufs in enumerate((own, core)):
            for b in range(3):
                self.start(bufs[b], low, low, high, 4 * half + b, sems)
            if low < cut:
                self.start(bufs[3], low, low, min(high, cut), 4 * half + 3, sems)
            if high > cut:
                at = max(low, cut)
                self.start(bufs[4], at - cut, at, high, 4 * half + 3, sems)

    def start(self, buf, source, low, high, b, sems):
        copy = pltpu.make_async_copy(
            buf.at[pl.ds(source, high - low)],
            self.scratch.at[b, pl.ds(low - self.low, high - low)],
            sems.at[len(self.copies)],
        )
        copy.start()
        self.copies.append(copy)

    def wait(self):
        for copy in self.copies:
            copy.wait()

    def one(self, b, at, rows=TILE):
        return self.scratch[b, at - self.low : at - self.low + rows, :]


def by_tiles(blocks, held, at, turned=False):
    return [
        dot(blocks[b], held.one(b, at), 1, 1 if turned else 0) for b in range(HOLD)
    ]


HELD_REFS = 10


LW, LQ, LV, LP, LC, LEND = 0, 128, 256, 384, 512, 768


def leaf_start_kernel(
    src, w, p, q, c, piv, tl, ranks_l, ranks_m, ranks_u, ranks_r,
    first, y0, plan, rows, hold,
):
    b = src[...]
    y = mm(b, w[...])
    v = q[:, TILE:]
    first[0:RHS, :] = mm(b, q[:, 0:TILE])
    first[RHS : 2 * RHS, :] = mm(y, v)
    first[2 * RHS :, :] = cross(p[...], v)
    y0[...] = y
    dest, label = split_target(tl[...], 13)
    plan[0:1, :] = dest.astype(F32)
    plan[1:2, :] = label
    plan[2:3, :] = leaf_slots(row_onehot(dest, 64))
    plan[3:8, :] = jnp.zeros((5, 2 * TILE), F32)
    found = []
    for ranks, groups, dim in (
        (ranks_l, 1, 1), (ranks_m, 16, 1), (ranks_u, 32, 0), (ranks_r, 64, 0),
    ):
        found += mask_rows(ranks, groups, dim)
    rows[...] = jnp.concatenate(found[0:7] + [piv[...]], axis=0)
    hold[LW:LQ, :] = w[...]
    hold[LQ:LV, :] = q[:, 0:TILE]
    hold[LV:LP, :] = v
    hold[LP:LC, :] = p[...]
    hold[LC:LEND, :] = c[...]


def pack_kernel(*refs):
    (sm, wm, pm, qm, vm, cm, tm), rest = refs[0:7], refs[7:]
    (su, wu, pu, qu, vu, cu, tu), rest = rest[0:7], rest[7:]
    (sr, wr, pr, qr, vr), rest = rest[0:5], rest[5:]
    pack_m, pack_u = rest
    for pack, s, wt, pt, qt, vt, ct, t in (
        (pack_m, sm, wm, pm, qm, vm, cm, tm),
        (pack_u, su, wu, pu, qu, vu, cu, tu),
    ):
        pack[SRC:WAT, :] = s[...]
        pack[WAT:QAT, :] = wt[...]
        pack[QAT:VAT, :] = qt[:, 0:TILE]
        pack[VAT:MISC, :] = qt[:, TILE:]
        at = iota((8, TILE), 0)
        pack[MISC:CAT, :] = jnp.where(
            at == 0,
            jnp.broadcast_to(vt[...], (8, TILE)),
            jnp.broadcast_to(t[...].astype(F32), (8, TILE)),
        )
        pack[CAT:PAT, :] = ct[...]
        pack[PAT:END, :] = pt[...]
    pack_u[END + SRC : END + WAT, :] = sr[...]
    pack_u[END + WAT : END + QAT, :] = wr[...]
    pack_u[END + QAT : END + RMISC, :] = qr[:, 0:TILE]
    pack_u[END + RMISC : END + RPAT, :] = jnp.broadcast_to(vr[...], (8, TILE))
    pack_u[END + RPAT : END + REND, :] = pr[...]


def cross_kernel(*refs):
    _, k1, k2, low, high, low_core, high_core = refs[HELD_REFS:]
    for source, kept in zip(refs[3:5] + refs[8:10], (low, high, low_core, high_core)):
        kept[...] = source[...]
    upper = Held(refs, END)
    root = Held(refs, END, END)
    k1[...] = cross(upper.all(PAT), upper.all(VAT))
    total = None
    for b in range(HOLD):
        p = root.one(b, RPAT)
        part = mm(p.T * root.one(b, RMISC, 1), p)
        total = part if total is None else total + part
    k2[...] = total


def leaf_picks(plan):
    dest = plan[0:1, :].astype(jnp.int32)
    place = lax.shift_right_logical(dest, 3) * 4 + jnp.bitwise_and(dest, 3)
    half = jnp.bitwise_and(lax.shift_right_logical(dest, 2), 1)
    hit = row_onehot(place, 4 * HOLD)
    return [hit * (half == h).astype(F32) for h in range(2)]


def leaf_up_kernel(s0, s1, s2, s3, y0, plan, rows, hold, out, z_out, zp_out, k_out):
    total = (s0[...] + s1[...]) + (s2[...] + s3[...])
    mh, mc = masks(rows, 0)
    k1 = total[2 * RHS :, :]
    hq = total[0:RHS, :] * mh
    wv = (total[RHS : 2 * RHS, :] + mm(hq, k1)) * mc
    e = -mmt(wv, hold[LC:LEND, :])
    both = jnp.concatenate([e, label_rows(plan[1:2, :])], axis=0)
    at = plan[2:3, :]
    parts = jnp.concatenate(
        [both * (at == float(k)).astype(F32) for k in range(SLOTS_LEAF)], axis=0
    )
    both = stacked(parts)
    sent = tall([fold(raw(both, pick.astype(BF16), 1, 1)) for pick in leaf_picks(plan)]).T
    for place in range(0, HOLD, 2):
        pairs = [sent[4 * at : 4 * at + 4, :] for at in (place, place + 1)]
        for at, part in zip((place, place + 1), pairs):
            twice = jnp.concatenate([part, part], axis=0)
            for copy in range(0, HOLD, 2):
                low = (at * HOLD + copy) * 4
                out[low : low + HOLD, :] = twice
    p = hold[LP:LC, :]
    z = (y0[...] + mmt(hq, p)) * rows[7:8, :]
    z_out[...] = z
    zp_out[...] = mm(z, p)
    k_out[...] = k1


def write_copies(ref, value):
    rows = value.shape[0]
    for i in range(ref.shape[0] // rows):
        ref[rows * i : rows * (i + 1), :] = value


def write_shares(ref, members, value, parts):
    step = ref.shape[0] // members
    rows = step - parts.shape[0] // min(members, 16)
    each = step - rows
    common = value.shape[0] == rows
    for i in range(members):
        low = step * i
        ref[low : low + rows, :] = value if common else value[rows * i : rows * (i + 1)]
        at = each * (i % 16)
        ref[low + rows : low + step, :] = parts[at : at + each]


def sum_rows(ref, step, low, high):
    total = ref[low:high, :]
    for i in range(1, ref.shape[0] // step):
        total = total + ref[step * i + low : step * i + high, :]
    return total


def stack_rows(ref, step, low, high, count):
    return jnp.concatenate(
        [ref[step * i + low : step * i + high, :] for i in range(count)], axis=0
    )


def enter_middle_kernel(*refs):
    got, part, y_out, upd_out, scratch, sems = refs[HELD_REFS:]
    held = Fetched(refs, MISC, SRC, VAT, scratch, sems)
    inc = received(got[...].T, True, 2 * TILE)
    held.wait()
    b = [held.one(j, SRC, RHS) + inc[RHS * j : RHS * (j + 1), 0:TILE] for j in range(HOLD)]
    write_copies(part, mm(lanes(b), held.all(QAT)))
    y_out[...] = lanes(by_tiles(b, held, WAT))
    upd_out[...] = inc[:, TILE:]


def middle_kernel(*refs):
    red, y0, rows, part, z_out, zp_out, scratch, sems = refs[HELD_REFS:]
    held = Fetched(refs, MISC, VAT, END, scratch, sems)
    mh, _ = masks(rows, 1)
    hq = sum_rows(red, RHS, 0, RHS) * mh
    held.wait()
    p, v = held.all(PAT), held.all(VAT)
    y = y0[...] + mmt(hq, p)
    write_shares(part, 8, mm(y, v), cross(p, v))
    z = y * lanes([held.one(b, MISC, 1) for b in range(HOLD)])
    z_out[...] = z
    zp_out[...] = mm(z, p)


def middle_up_kernel(*refs):
    red, upd, rows, k1, out, k_out, scratch, copied, sems = refs[HELD_REFS:]
    held = Fetched(refs, MISC, MISC, PAT, copied, sems)
    _, mc = masks(rows, 1)
    total = sum_rows(red, 3 * RHS, 0, 3 * RHS)
    k_out[...] = total[RHS:, :]
    wv = total[0:RHS, :] * mc
    held.wait()
    e = cut_lanes(mmt(wv, held.all(CAT)))
    upds = cut_tall(upd[...])
    targets = held.misc(MISC, 1).astype(jnp.int32)
    sent = messages([u - v for u, v in zip(upds, e)], targets, 14, 128, scratch)
    write_shares(out, 16, sent, k1[...])


def enter_upper_kernel(*refs):
    got, part, y_out, upd_out = refs[HELD_REFS:]
    held = Held(refs, END)
    k1 = sum_rows(got, 2 * RHS, RHS, 2 * RHS)
    inc = received(stack_rows(got, 2 * RHS, 0, RHS, 16).T, False, 2 * TILE)
    b = [held.one(j, SRC, RHS) + inc[RHS * j : RHS * (j + 1), 0:TILE] for j in range(HOLD)]
    y = lanes(by_tiles(b, held, WAT))
    write_copies(part, tall([mm(lanes(b), held.all(QAT)), mm(y, held.all(VAT)), k1]))
    y_out[...] = y
    upd_out[...] = inc[:, TILE:]


def upper_up_kernel(*refs):
    red, y0, upd, rows, k2, out, z_out, zp_out, k_out, scratch = refs[HELD_REFS:]
    held = Held(refs, END)
    total = sum_rows(red, 3 * RHS, 0, 2 * RHS)
    k1 = stack_rows(red, 3 * RHS, 2 * RHS, 3 * RHS, 16)
    k_out[...] = k1
    mh, mc = masks(rows, 2)
    hq = total[0:RHS, :] * mh
    wv = (total[RHS:, :] + mm(hq, k1)) * mc
    e = cut_lanes(mmt(wv, held.all(CAT)))
    upds = cut_tall(upd[...])
    targets = held.misc(MISC, 1).astype(jnp.int32)
    sent = messages([u - v for u, v in zip(upds, e)], targets, 15, 256, scratch)
    write_shares(out, 32, sent, k2[...])
    p = held.all(PAT)
    y = y0[...] + mmt(hq, p)
    z = y * lanes([held.one(b, MISC, 1) for b in range(HOLD)])
    z_out[...] = z
    zp_out[...] = mm(z, p)


def enter_root_kernel(*refs):
    got, part, y_out = refs[HELD_REFS:]
    held = Held(refs, END, END)
    k2 = sum_rows(got, 2 * RHS, RHS, 2 * RHS)
    inc = received(stack_rows(got, 2 * RHS, 0, RHS, 32).T, False, TILE)
    b = [held.one(j, SRC, RHS) + inc[RHS * j : RHS * (j + 1)] for j in range(HOLD)]
    y = lanes(by_tiles(b, held, WAT))
    z = y * lanes([held.one(j, RMISC, 1) for j in range(HOLD)])
    write_copies(part, tall([mm(lanes(b), held.all(QAT)), mm(z, held.all(RPAT)), k2]))
    y_out[...] = y


def root_kernel(*refs):
    red, y0, rows, got, answer, reply = refs[HELD_REFS:]
    held = Held(refs, END, END)
    total = sum_rows(red, 3 * RHS, 0, 2 * RHS)
    k2 = stack_rows(red, 3 * RHS, 2 * RHS, 3 * RHS, 16)
    mh = rows[6:7, :]
    hq = total[0:RHS, :] * mh
    pr = (total[RHS:, :] + mm(hq, k2)) * mh
    turned = stack_rows(got, 2 * RHS, 0, RHS, 32).T
    r = y0[...] + mmt(hq, held.all(RPAT))
    r = r * lanes([held.one(j, RMISC, 1) for j in range(HOLD)])
    x = by_tiles(cut_lanes(r), held, WAT, True)
    low = cut_lanes(mmt(pr, held.all(QAT)))
    x = [u + v for u, v in zip(x, low)]
    answer[...] = x[0]
    reply[...] = replies(turned, False, tall(x))


def fetch_kernel(shift, cut, *refs):
    back, *tails, part, xu_out, scratch = refs[HELD_REFS:]
    held = Held(refs, cut)
    targets = held.misc(MISC, 1).astype(jnp.int32)
    xu = fetched(back[...], targets, shift, scratch)
    write_copies(part, tall([mm(lanes(xu), held.all(CAT))] + [ref[...] for ref in tails]))
    xu_out[...] = tall(xu)


def solve_held(total, z, k1, held, mh, mc):
    s = total[0:RHS, :] * mc
    r = z - mmt(s, held.all(VAT))
    pr = (total[RHS:, :] - mmt(s, k1)) * mh
    x = by_tiles(cut_lanes(r), held, WAT, True)
    low = cut_lanes(mmt(pr, held.all(QAT)))
    return [u + v for u, v in zip(x, low)]


def down_upper_kernel(*refs):
    red, z, rows, xu, got, k1, answer, reply = refs[HELD_REFS:]
    held = Held(refs, END)
    mh, mc = masks(rows, 2)
    total = sum_rows(red, 2 * RHS, 0, 2 * RHS)
    turned = stack_rows(got, 2 * RHS, 0, RHS, 16).T
    x = solve_held(total, z[...], k1[...], held, mh, mc)
    answer[...] = x[0]
    reply[...] = replies(turned, False, jnp.concatenate([tall(x), xu[...]], axis=1))


def down_middle_kernel(*refs):
    red, z, rows, xu, got, answer, reply = refs[HELD_REFS:]
    held = Held(refs, MISC)
    mh, mc = masks(rows, 1)
    total = sum_rows(red, 4 * RHS, 0, 2 * RHS)
    k1 = stack_rows(red, 4 * RHS, 2 * RHS, 4 * RHS, 8)
    me = own_number()
    pair = lax.shift_right_logical(me, 1)
    odd = jnp.bitwise_and(me, 1) == 1
    asked = []
    for i in range(HOLD):
        two = got[pl.ds(pl.multiple_of((4 * i + pair) * HOLD, HOLD), HOLD), :]
        asked.append(jnp.where(odd, two[4:], two[0:4]))
    x = solve_held(total, z[...], k1, held, mh, mc)
    answer[...] = x[0]
    both = jnp.concatenate([tall(x), xu[...]], axis=1)
    reply[...] = replies(tall(asked).T, True, both)


def fetch_leaf_kernel(back, plan, hold, zp, part):
    turned = back[...].T
    both = None
    for h, pick in enumerate(leaf_picks(plan)):
        first = h * SLOTS_LEAF
        slots = tall(
            [turned[SLOT * k : SLOT * k + RHS, :] for k in range(first, first + SLOTS_LEAF)]
        )
        one = fold(raw(stacked(slots), pick.astype(BF16), 1, 0))
        both = one if both is None else both + one
    at = plan[2:3, :]
    xu = None
    for k in range(SLOTS_LEAF):
        one = both[RHS * k : RHS * (k + 1), :] * (at == float(k)).astype(F32)
        xu = one if xu is None else xu + one
    part[0:RHS, :] = mm(xu, hold[LC:LEND, :])
    part[RHS:, :] = zp[...]


def leaf_kernel(s0, s1, s2, s3, z, k1, hold, rows, answer):
    total = (s0[...] + s1[...]) + (s2[...] + s3[...])
    mh, mc = masks(rows, 0)
    s = total[0:RHS, :] * mc
    r = z[...] - mmt(s, hold[LV:LP, :])
    pr = (total[RHS:, :] - mmt(s, k1[...])) * mh
    answer[...] = mmt(r, hold[LW:LQ, :]) + mmt(pr, hold[LQ:LV, :])


def run(kernel, shapes, *args, answer=False, inputs=False, scratch=(), copied=0):
    outs = [pltpu.VMEM(s, F32) for s in shapes]
    if answer:
        outs[0] = jax.ShapeDtypeStruct(shapes[0], F32)
    options = {}
    scratch = [pltpu.VMEM(s, F32) for s in scratch]
    if copied:
        scratch += [pltpu.VMEM((HOLD, copied, TILE), F32), pltpu.SemaphoreType.DMA((12,))]
        rest = [pltpu.with_memory_space_constraint(a, pltpu.VMEM) for a in args[HELD_REFS:]]
        far = [pltpu.with_memory_space_constraint(a, pltpu.HBM) for a in args[:HELD_REFS]]
        args = far + rest
        options["in_specs"] = [pl.BlockSpec(memory_space=pltpu.HBM)] * HELD_REFS + [
            pl.BlockSpec(memory_space=pltpu.VMEM) for _ in rest
        ]
    elif not inputs:
        args = [pltpu.with_memory_space_constraint(a, pltpu.VMEM) for a in args]
    return pl.pallas_call(
        kernel,
        out_shape=outs[0] if len(outs) == 1 else outs,
        scratch_shapes=scratch,
        compiler_params=None if inputs else pltpu.CompilerParams(vmem_limit_bytes=16 << 20),
        **options,
    )(*args)


def after(done, *values):
    return lax.optimization_barrier((*values, done))[:-1]


def swap(value, axis, mask):
    pairs = [(s, s ^ mask) for s in range(lax.axis_size(axis))]
    return lax.ppermute(value, axis, pairs)


def shift(value, step):
    size = lax.axis_size("grid")
    return lax.ppermute(value, "grid", [(s, (s + step) % size) for s in range(size)])


def four(value, axis, unit):
    return [value] + [swap(value, axis, unit * m) for m in (1, 2, 3)]


def together(*values):
    return lax.optimization_barrier(values)


def between(value, members):
    size = lax.axis_size("leaf")
    groups = [
        [start + core + 2 * i for i in range(members)]
        for start in range(0, size, 2 * members)
        for core in range(2)
    ]
    return lax.all_to_all(
        value, "leaf", split_axis=0, concat_axis=0, tiled=True, axis_index_groups=groups
    )


def route_leaf(value):
    size = lax.axis_size("leaf") * lax.axis_size("grid")
    groups = [list(range(g, g + 64)) for g in range(0, size, 64)]
    return lax.all_to_all(
        value,
        ("leaf", "grid"),
        split_axis=0,
        concat_axis=0,
        tiled=True,
        axis_index_groups=groups,
    )


def shards(
    src_l, w_l, p_l, q_l, piv_l, c_l, ranks_l, t_l,
    src_m, w_m, p_m, q_m, piv_m, c_m, ranks_m, t_m,
    src_u, w_u, p_u, q_u, piv_u, c_u, ranks_u, t_u,
    src_r, w_r, p_r, q_r, piv_r, ranks_r,
):
    ranks_l, ranks_m = ranks_l.T, ranks_m.T
    t_l, t_m, t_u = (t.reshape(1, -1) for t in (t_l, t_m, t_u))
    piv_l, piv_m, piv_u, piv_r = (v.reshape(1, -1) for v in (piv_l, piv_m, piv_u, piv_r))
    row = (RHS, TILE)
    pair = (2 * RHS, TILE)
    flat = (RHS, HOLD * TILE)
    high = (HOLD * RHS, TILE)

    first, y_l, plan, rows, hold = run(
        leaf_start_kernel,
        [(2 * RHS + TILE, TILE), row, (RHS, 2 * TILE), row, (LEND, TILE)],
        src_l, w_l, p_l, q_l, c_l, piv_l, t_l, ranks_l, ranks_m, ranks_u, ranks_r,
        inputs=True,
    )
    sums = four(first, "grid", 1)
    pack_m, pack_u = run(
        pack_kernel, [(END, TILE), (END + REND, TILE)],
        src_m, w_m, p_m, q_m, piv_m, c_m, t_m,
        src_u, w_u, p_u, q_u, piv_u, c_u, t_u,
        src_r, w_r, p_r, q_r, piv_r,
        inputs=True,
    )
    m_core, u_core = swap(pack_m, "leaf", 1), swap(pack_u, "leaf", 1)
    *sums, pack_m = together(*sums, pack_m)
    m_prev = shift(pack_m, 1)
    m_next = shift(pack_m, -1)
    out, z_l, zp_l, k_l = run(
        leaf_up_kernel,
        [(64 * 4, LANES), row, row, (TILE, TILE)],
        *sums, y_l, plan, rows, hold,
    )
    got_m = route_leaf(out)
    m_prev, m_next = after(got_m, m_prev, m_next)
    m_low, m_high = shift(m_prev[:MISC], 1), shift(m_next[MISC:], -1)
    m_prev_core, m_next_core = swap(m_prev, "leaf", 1), swap(m_next, "leaf", 1)
    held_m = (
        pack_m, m_prev, m_next, m_low, m_high,
        m_core, m_prev_core, m_next_core, swap(m_low, "leaf", 1), swap(m_high, "leaf", 1),
    )

    part, y_m, upd_m = run(
        enter_middle_kernel, [(8 * RHS, TILE), flat, high], *held_m, got_m,
        copied=VAT - SRC,
    )
    (pack_u,) = after(part, pack_u)
    u_prev = shift(pack_u, 1)
    u_next = shift(pack_u, -1)
    red = between(part, 8)
    u_prev, u_next = after(red, u_prev, u_next)
    u_low, u_high = shift(u_prev[:END], 1), shift(u_next[END:], -1)
    u_prev_core, u_next_core = swap(u_prev, "leaf", 1), swap(u_next, "leaf", 1)
    part, z_m, zp_m = run(
        middle_kernel, [(8 * 3 * RHS, TILE), flat, row], *held_m, red, y_m, rows,
        copied=END - VAT,
    )
    u_low, u_high = after(part, u_low, u_high)
    held_u = (
        pack_u, u_prev, u_next, u_low, u_high,
        u_core, u_prev_core, u_next_core, swap(u_low, "leaf", 1), swap(u_high, "leaf", 1),
    )
    red = between(part, 8)
    k_u, k_r, *opposite = run(
        cross_kernel, [(TILE, TILE)] * 2 + [(END, TILE), (REND, TILE)] * 2, *held_u, red
    )
    held_u = (*held_u[:3], *opposite[:2], *held_u[5:8], *opposite[2:])
    out, k_m = run(
        middle_up_kernel, [(16 * 2 * RHS, LANES), pair],
        *held_m, red, upd_m, rows, k_u, scratch=[(LANES, 128)], copied=PAT - MISC,
    )
    got_u = between(out, 16)

    part, y_u, upd_u = run(
        enter_upper_kernel, [(16 * 3 * RHS, TILE), flat, high], *held_u, got_u
    )
    red = between(part, 16)
    out, z_u, zp_u, k_u = run(
        upper_up_kernel, [(32 * 2 * RHS, LANES), flat, row, (TILE, TILE)],
        *held_u, red, y_u, upd_u, rows, k_r, scratch=[(LANES, 256)],
    )
    got_r = between(out, 32)

    part, y_r = run(enter_root_kernel, [(32 * 3 * RHS, TILE), flat], *held_u, got_r)
    red = between(part, 32)
    x_r, out = run(
        root_kernel, [row, (256, LANES)], *held_u, red, y_r, rows, got_r, answer=True
    )

    back = between(out, 32)
    part, xu = run(
        functools.partial(fetch_kernel, 15, END), [(16 * 2 * RHS, TILE), high],
        *held_u, back, zp_u, scratch=[(LANES, 256)],
    )
    red = between(part, 16)
    x_u, out = run(
        down_upper_kernel, [row, (128, LANES)],
        *held_u, red, z_u, rows, xu, got_u, k_u, answer=True,
    )

    back = between(out, 16)
    part, xu = run(
        functools.partial(fetch_kernel, 14, MISC), [(8 * 4 * RHS, TILE), high],
        *held_m, back, zp_m, k_m, scratch=[(LANES, 128)],
    )
    red = between(part, 8)
    x_m, out = run(
        down_middle_kernel, [row, (32, LANES)],
        *held_m, red, z_m, rows, xu, got_m, answer=True,
    )

    back = between(out, 8)
    part = run(fetch_leaf_kernel, [pair], back, plan, hold, zp_l)
    x_l = run(leaf_kernel, [row], *four(part, "grid", 1), z_l, k_l, hold, rows, answer=True)
    return (x_l, x_m, x_u, x_r)


def solution(mesh):
    both = ("leaf", "grid")
    wide = P(None, both)
    deep = P(both, None)
    line = P(both)
    level = (wide, deep, deep, deep, line, deep, P(), line)
    in_specs = level * 3 + (wide, deep, deep, deep, line, P())
    return jax.shard_map(
        shards, mesh=mesh, in_specs=in_specs, out_specs=(wide,) * 4, check_vma=False
    )
```

profile of v0, /device:TPU:2, one launch (start us, length us, event | category | flops | bytes accessed | tf_op | source)
XLA Modules:
  0.0 227.9 jit_solution(11883257807392646134)
XLA Ops:
  0.6 1.5 shard_map.309
  2.1 1.6 collective-permute-start.2
  3.7 2.8 %collective-permute-start.1 = (f32[144,128]{1,0:T(8,128)S(1)}, f32[144,128]{1,0:T(8,128)S(1)}, u32[]{:S(2)}, u32[]{:S(2)}) collective-permute-start(f32[144,128]{1,0:T(8,128)S(1)} %get-tuple-element.63.s0), channel_id=1, source_target_pairs={{0,2},{1,3},{2,0},{3,1},{4,6},{5,7},{6,4},{7,5},{8,10},{9,11},{10,... | collective-permute-start | bytes 221192 | tf_op jit(solution)/shard_map/ppermute | solution.py:638
  6.5 0.0 collective-permute-start
  6.5 1.3 shard_map.310
  7.9 2.0 collective-permute-done.1.s2
  9.8 1.0 collective-permute-done.s1
  10.9 0.8 collective-permute-start.4
  11.7 1.2 collective-permute-start.3
  12.9 0.5 shard_map.311
  13.5 0.0 copy-start.28
  13.5 21.9 %all_to_all.132 = f32[64,4,128]{2,1,0:T(4,128)S(1)} all-to-all(f32[64,4,128]{2,1,0:T(4,128)S(1)} %bitcast.51), channel_id=1, replica_groups={{0,1,2,3,4,5,6,7,8,9,10,11,12,13,14,15,16,17,18,19,20,21,22,23,24,25,26..., dimensions={0} | all-to-all | bytes 262144 | tf_op jit(solution)/shard_map/all_to_all | solution.py:669
  35.4 0.0 collective-permute-done.4.refs_2_
  35.4 0.8 collective-permute-start.5
  36.2 0.5 collective-permute-start.8
  36.7 0.0 collective-permute-start.9
  36.8 1.4 collective-permute-start.6
  38.2 3.1 %collective-permute-done.5.refs_3_ = f32[392,128]{1,0:T(8,128)S(1)} collective-permute-done((f32[392,128]{1,0:T(8,128)S(1)}, f32[392,128]{1,0:T(8,128)S(1)}, u32[]{:S(2)}, u32[]{:S(2)}) %collective-permute-start.5) | collective-permute-done | bytes 200736 | tf_op jit(solution)/shard_map/ppermute | solution.py:643
  41.2 1.6 collective-permute-done.6.refs_4_
  42.9 1.3 collective-permute-done.11.refs_9_
  44.3 0.6 copy-done.20
  44.8 0.2 copy-done.8
  45.0 0.1 copy-done.10
  45.1 0.7 copy-done.14
  45.8 2.0 shard_map.312
  47.8 0.6 copy-done.22
  48.4 1.5 collective-permute-start.13
  49.9 0.5 collective-permute-start.12
  50.4 10.4 %all_to_all.133 = f32[8,8,128]{2,1,0:T(8,128)S(1)} all-to-all(f32[8,8,128]{2,1,0:T(8,128)S(1)} %bitcast.58), channel_id=1, replica_groups={{0,8,16,24,32,40,48,56},{4,12,20,28,36,44,52,60},{64,72,80,88,96,104,11..., dimensions={0} | all-to-all | bytes 65536 | tf_op jit(solution)/shard_map/all_to_all | solution.py:661
  60.8 1.9 collective-permute-done.13.refs_2_
  62.7 3.2 %collective-permute-done.12.refs_1_ = f32[1056,128]{1,0:T(8,128)S(1)} collective-permute-done((f32[1056,128]{1,0:T(8,128)S(1)}, f32[1056,128]{1,0:T(8,128)S(1)}, u32[]{:S(2)}, u32[]{:S(2)}) %collective-permute-start.12) | collective-permute-done | bytes 540704 | tf_op jit(solution)/shard_map/ppermute | solution.py:643
  65.9 0.3 collective-permute-start.14
  66.2 3.0 %collective-permute-start.15 = (f32[400,128]{1,0:T(8,128)S(1)}, f32[400,128]{1,0:T(8,128)}, u32[]{:S(2)}, u32[]{:S(2)}) collective-permute-start(f32[400,128]{1,0:T(8,128)S(1)} %slice.15), channel_id=1, source_target_pairs={{0,3},{1,0},{2,1},{3,2},{4,7},{5,4},{6,5},{7,6},{8,11},{9,8},{10,9... | collective-permute-start | bytes 614408 | tf_op jit(solution)/shard_map/ppermute | solution.py:643
  69.3 0.5 collective-permute-start.17
  69.8 2.9 %shard_map.313 = (f32[192,128]{1,0:T(8,128)}, f32[8,1024]{1,0:T(8,128)S(1)}, f32[8,128]{1,0:T(8,128)S(1)}) custom-call(f32[656,128]{1,0:T(8,128)} %copy-done.4, f32[656,128]{1,0:T(8,128)} %copy-done, f32[656,128]{1,0:T(8,128)} %copy-done.2, f32[392,128]{1,0:T(8,128)} %copy-done.12, f32[264,128]{1,0:T(8,128)} %copy-done.18, f32[656,128]{1,0:T(8,128)} %copy-done.6, ...), custom_call_target="tpu_custom_call" | custom-call | tf_op jit(solution)/shard_map/pallas_call | solution.py:623
  72.7 0.6 collective-permute-done.15.refs_4_
  73.3 3.0 %collective-permute-done.14.refs_3_ = f32[656,128]{1,0:T(8,128)} collective-permute-done((f32[656,128]{1,0:T(8,128)S(1)}, f32[656,128]{1,0:T(8,128)}, u32[]{:S(2)}, u32[]{:S(2)}) %collective-permute-start.14) | collective-permute-done | bytes 335904 | tf_op jit(solution)/shard_map/ppermute | solution.py:643
  76.3 0.5 collective-permute-start.20
  76.8 3.4 %all-to-all-start.2 = ((f32[8,24,128]{2,1,0:T(8,128)}), f32[8,24,128]{2,1,0:T(8,128)S(1)}, u32[]{:S(2)}, u32[]{:S(2)}) async-start(f32[8,24,128]{2,1,0:T(8,128)} %bitcast.13), calls=%async_computation.2 | async-start | bytes 196608 | tf_op jit(solution)/shard_map/all_to_all | solution.py:661
  80.2 8.8 %all-to-all-done.2 = f32[8,24,128]{2,1,0:T(8,128)S(1)} async-done(((f32[8,24,128]{2,1,0:T(8,128)}), f32[8,24,128]{2,1,0:T(8,128)S(1)}, u32[]{:S(2)}, u32[]{:S(2)}) %all-to-all-start.2) | async-done | bytes 98336 | tf_op jit(solution)/shard_map/all_to_all | solution.py:661
  89.0 2.0 shard_map.314
  91.0 1.8 shard_map.315
  92.8 11.3 %all_to_all.134 = f32[16,16,128]{2,1,0:T(8,128)S(1)} all-to-all(f32[16,16,128]{2,1,0:T(8,128)S(1)} %bitcast.52), channel_id=1, replica_groups={{0,8,16,24,32,40,48,56,64,72,80,88,96,104,112,120},{4,12,20,28,36,44,52..., dimensions={0} | all-to-all | bytes 262144 | tf_op jit(solution)/shard_map/all_to_all | solution.py:661
  104.2 1.0 shard_map.316
  105.2 11.8 %all_to_all.135 = f32[16,24,128]{2,1,0:T(8,128)S(1)} all-to-all(f32[16,24,128]{2,1,0:T(8,128)S(1)} %bitcast.49), channel_id=1, replica_groups={{0,8,16,24,32,40,48,56,64,72,80,88,96,104,112,120},{4,12,20,28,36,44,52..., dimensions={0} | all-to-all | bytes 393216 | tf_op jit(solution)/shard_map/all_to_all | solution.py:661
  117.0 0.9 shard_map.317
  117.9 17.1 %all_to_all.136 = f32[32,16,128]{2,1,0:T(8,128)S(1)} all-to-all(f32[32,16,128]{2,1,0:T(8,128)S(1)} %bitcast.48), channel_id=1, replica_groups={{0,8,16,24,32,40,48,56,64,72,80,88,96,104,112,120,128,136,144,152,160,1..., dimensions={0} | all-to-all | bytes 524288 | tf_op jit(solution)/shard_map/all_to_all | solution.py:661
  135.0 0.8 shard_map.318
  135.8 15.9 %all_to_all.137 = f32[32,24,128]{2,1,0:T(8,128)S(1)} all-to-all(f32[32,24,128]{2,1,0:T(8,128)S(1)} %bitcast.46), channel_id=1, replica_groups={{0,8,16,24,32,40,48,56,64,72,80,88,96,104,112,120,128,136,144,152,160,1..., dimensions={0} | all-to-all | bytes 786432 | tf_op jit(solution)/shard_map/all_to_all | solution.py:661
  151.6 1.3 shard_map.319
  153.0 15.5 %all_to_all.138 = f32[32,8,128]{2,1,0:T(8,128)S(1)} all-to-all(f32[32,8,128]{2,1,0:T(8,128)S(1)} %bitcast.53), channel_id=1, replica_groups={{0,8,16,24,32,40,48,56,64,72,80,88,96,104,112,120,128,136,144,152,160,1..., dimensions={0} | all-to-all | bytes 262144 | tf_op jit(solution)/shard_map/all_to_all | solution.py:661
  168.5 0.4 shard_map.320
  169.0 11.2 %all_to_all.139 = f32[16,16,128]{2,1,0:T(8,128)S(1)} all-to-all(f32[16,16,128]{2,1,0:T(8,128)S(1)} %bitcast.55), channel_id=1, replica_groups={{0,8,16,24,32,40,48,56,64,72,80,88,96,104,112,120},{4,12,20,28,36,44,52..., dimensions={0} | all-to-all | bytes 262144 | tf_op jit(solution)/shard_map/all_to_all | solution.py:661
  180.2 1.4 shard_map.321
  181.6 11.7 %all_to_all.140 = f32[16,8,128]{2,1,0:T(8,128)S(1)} all-to-all(f32[16,8,128]{2,1,0:T(8,128)S(1)} %bitcast.56), channel_id=1, replica_groups={{0,8,16,24,32,40,48,56,64,72,80,88,96,104,112,120},{4,12,20,28,36,44,52..., dimensions={0} | all-to-all | bytes 131072 | tf_op jit(solution)/shard_map/all_to_all | solution.py:661
  193.3 0.4 shard_map.322
  193.8 12.6 %all_to_all.141 = f32[8,32,128]{2,1,0:T(8,128)S(1)} all-to-all(f32[8,32,128]{2,1,0:T(8,128)S(1)} %bitcast.54), channel_id=1, replica_groups={{0,8,16,24,32,40,48,56},{4,12,20,28,36,44,52,60},{64,72,80,88,96,104,11..., dimensions={0} | all-to-all | bytes 262144 | tf_op jit(solution)/shard_map/all_to_all | solution.py:661
  206.4 1.3 shard_map.323
  207.7 10.3 %all_to_all.142 = f32[8,4,128]{2,1,0:T(4,128)S(1)} all-to-all(f32[8,4,128]{2,1,0:T(4,128)S(1)} %bitcast.59), channel_id=1, replica_groups={{0,8,16,24,32,40,48,56},{4,12,20,28,36,44,52,60},{64,72,80,88,96,104,11..., dimensions={0} | all-to-all | bytes 32768 | tf_op jit(solution)/shard_map/all_to_all | solution.py:661
  217.9 0.3 shard_map.324.s0
  218.3 5.0 %collective-permute-start.22 = (f32[16,128]{1,0:T(8,128)S(1)}, f32[16,128]{1,0:T(8,128)S(1)}, u32[]{:S(2)}, u32[]{:S(2)}) collective-permute-start(f32[16,128]{1,0:T(8,128)S(1)} %shard_map.324.s0), channel_id=1, source_target_pairs={{0,2},{1,3},{2,0},{3,1},{4,6},{5,7},{6,4},{7,5},{8,10},{9,11},{10,... | collective-permute-start | bytes 24584 | tf_op jit(solution)/shard_map/ppermute | solution.py:638
  223.3 1.6 collective-permute-done.22.s2
  224.9 2.0 collective-permute-done.21.s1
  227.0 0.9 shard_map.325
  (78 shorter events, 0.2 us)
Async XLA Ops:
  2.1 10.8 %copy-start.16 = (f32[768,128]{1,0:T(8,128)}, f32[768,128]{1,0:T(8,128)S(1)}, u32[]{:S(2)}) copy-start(f32[768,128]{1,0:T(8,128)S(1)} %get-tuple-element.70.hold) | copy-start | bytes 1179652
  2.1 5.8 %collective-permute-start.2 = (f32[144,128]{1,0:T(8,128)S(1)}, f32[144,128]{1,0:T(8,128)S(1)}, u32[]{:S(2)}, u32[]{:S(2)}) collective-permute-start(f32[144,128]{1,0:T(8,128)S(1)} %get-tuple-element.63.s0), channel_id=1, source_target_pairs={{0,3},{1,2},{2,1},{3,0},{4,7},{5,6},{6,5},{7,4},{8,11},{9,10},{10,... | collective-permute-start | bytes 221192 | tf_op jit(solution)/shard_map/ppermute | solution.py:638
  3.7 6.1 %collective-permute-start.1 = (f32[144,128]{1,0:T(8,128)S(1)}, f32[144,128]{1,0:T(8,128)S(1)}, u32[]{:S(2)}, u32[]{:S(2)}) collective-permute-start(f32[144,128]{1,0:T(8,128)S(1)} %get-tuple-element.63.s0), channel_id=1, source_target_pairs={{0,2},{1,3},{2,0},{3,1},{4,6},{5,7},{6,4},{7,5},{8,10},{9,11},{10,... | collective-permute-start | bytes 221192 | tf_op jit(solution)/shard_map/ppermute | solution.py:638
  6.5 4.4 %collective-permute-start = (f32[144,128]{1,0:T(8,128)S(1)}, f32[144,128]{1,0:T(8,128)S(1)}, u32[]{:S(2)}, u32[]{:S(2)}) collective-permute-start(f32[144,128]{1,0:T(8,128)S(1)} %get-tuple-element.63.s0), channel_id=1, source_target_pairs={{0,1},{1,0},{2,3},{3,2},{4,5},{5,4},{6,7},{7,6},{8,9},{9,8},{10,11... | collective-permute-start | bytes 221192 | tf_op jit(solution)/shard_map/ppermute | solution.py:638
  7.9 28.4 %copy-start.4 = (f32[656,128]{1,0:T(8,128)}, f32[656,128]{1,0:T(8,128)S(1)}, u32[]{:S(2)}) copy-start(f32[656,128]{1,0:T(8,128)S(1)} %get-tuple-element.62.refs_0_) | copy-start | bytes 1007620
  10.9 24.5 %collective-permute-start.4 = (f32[656,128]{1,0:T(8,128)S(1)}, f32[656,128]{1,0:T(8,128)S(1)}, u32[]{:S(2)}, u32[]{:S(2)}) collective-permute-start(f32[656,128]{1,0:T(8,128)S(1)} %get-tuple-element.62.refs_0_), channel_id=1, source_target_pairs={{0,3},{1,0},{2,1},{3,2},{4,7},{5,4},{6,5},{7,6},{8,11},{9,8},{10,9... | collective-permute-start | bytes 1007624 | tf_op jit(solution)/shard_map/ppermute | solution.py:643
  11.7 23.7 %collective-permute-start.3 = (f32[656,128]{1,0:T(8,128)S(1)}, f32[656,128]{1,0:T(8,128)S(1)}, u32[]{:S(2)}, u32[]{:S(2)}) collective-permute-start(f32[656,128]{1,0:T(8,128)S(1)} %get-tuple-element.62.refs_0_), channel_id=1, source_target_pairs={{0,1},{1,2},{2,3},{3,0},{4,5},{5,6},{6,7},{7,4},{8,9},{9,10},{10,1... | collective-permute-start | bytes 1007624 | tf_op jit(solution)/shard_map/ppermute | solution.py:643
  13.5 21.9 %copy-start.26 = (f32[8,128]{1,0:T(8,128)}, f32[8,128]{1,0:T(8,128)S(1)}, u32[]{:S(2)}) copy-start(f32[8,128]{1,0:T(8,128)S(1)} %get-tuple-element.111.z) | copy-start | bytes 12292
  13.5 21.9 %copy-start.28 = (f32[8,128]{1,0:T(8,128)}, f32[8,128]{1,0:T(8,128)S(1)}, u32[]{:S(2)}) copy-start(f32[8,128]{1,0:T(8,128)S(1)} %get-tuple-element.110.zp) | copy-start | bytes 12292
  35.4 1.4 copy-start.2
  35.4 1.4 copy-start
  35.4 5.8 %collective-permute-start.5 = (f32[392,128]{1,0:T(8,128)S(1)}, f32[392,128]{1,0:T(8,128)S(1)}, u32[]{:S(2)}, u32[]{:S(2)}) collective-permute-start(f32[392,128]{1,0:T(8,128)S(1)} %slice.12), channel_id=1, source_target_pairs={{0,1},{1,2},{2,3},{3,0},{4,5},{5,6},{6,7},{7,4},{8,9},{9,10},{10,1... | collective-permute-start | bytes 602120 | tf_op jit(solution)/shard_map/ppermute | solution.py:643
  36.2 6.6 %collective-permute-start.7 = (f32[656,128]{1,0:T(8,128)S(1)}, f32[656,128]{1,0:T(8,128)S(1)}, u32[]{:S(2)}, u32[]{:S(2)}) collective-permute-start(f32[656,128]{1,0:T(8,128)S(1)} %get-tuple-element.62.refs_0_), channel_id=1, source_target_pairs={{0,4},{4,0},{8,12},{12,8},{16,20},{20,16},{24,28},{28,24},{32,36},... | collective-permute-start | bytes 1007624 | tf_op jit(solution)/shard_map/ppermute | solution.py:638
  36.2 8.0 %collective-permute-start.8 = (f32[656,128]{1,0:T(8,128)S(1)}, f32[656,128]{1,0:T(8,128)S(1)}, u32[]{:S(2)}, u32[]{:S(2)}) collective-permute-start(f32[656,128]{1,0:T(8,128)S(1)} %collective-permute-done.3.refs_1_), channel_id=1, source_target_pairs={{0,4},{4,0},{8,12},{12,8},{16,20},{20,16},{24,28},{28,24},{32,36},... | collective-permute-start | bytes 1007624 | tf_op jit(solution)/shard_map/ppermute | solution.py:638
  36.7 7.5 %collective-permute-start.9 = (f32[656,128]{1,0:T(8,128)S(1)}, f32[656,128]{1,0:T(8,128)S(1)}, u32[]{:S(2)}, u32[]{:S(2)}) collective-permute-start(f32[656,128]{1,0:T(8,128)S(1)} %collective-permute-done.4.refs_2_), channel_id=1, source_target_pairs={{0,4},{4,0},{8,12},{12,8},{16,20},{20,16},{24,28},{28,24},{32,36},... | collective-permute-start | bytes 1007624 | tf_op jit(solution)/shard_map/ppermute | solution.py:638
  36.8 6.1 %collective-permute-start.6 = (f32[264,128]{1,0:T(8,128)S(1)}, f32[264,128]{1,0:T(8,128)S(1)}, u32[]{:S(2)}, u32[]{:S(2)}) collective-permute-start(f32[264,128]{1,0:T(8,128)S(1)} %slice.13), channel_id=1, source_target_pairs={{0,3},{1,0},{2,1},{3,2},{4,7},{5,4},{6,5},{7,6},{8,11},{9,8},{10,9... | collective-permute-start | bytes 405512 | tf_op jit(solution)/shard_map/ppermute | solution.py:643
  41.2 3.0 %copy-start.12 = (f32[392,128]{1,0:T(8,128)}, f32[392,128]{1,0:T(8,128)S(1)}, u32[]{:S(2)}) copy-start(f32[392,128]{1,0:T(8,128)S(1)} %collective-permute-done.5.refs_3_) | copy-start | bytes 602116
  41.2 3.0 %collective-permute-start.10 = (f32[392,128]{1,0:T(8,128)S(1)}, f32[392,128]{1,0:T(8,128)S(1)}, u32[]{:S(2)}, u32[]{:S(2)}) collective-permute-start(f32[392,128]{1,0:T(8,128)S(1)} %collective-permute-done.5.refs_3_), channel_id=1, source_target_pairs={{0,4},{4,0},{8,12},{12,8},{16,20},{20,16},{24,28},{28,24},{32,36},... | collective-permute-start | bytes 602120 | tf_op jit(solution)/shard_map/ppermute | solution.py:638
  42.8 1.4 copy-start.18
  42.8 1.4 collective-permute-start.11
  42.9 1.4 copy-start.6
  44.2 0.6 copy-start.20
  44.2 0.8 copy-start.8
  44.2 0.9 copy-start.10
  45.1 0.7 copy-start.14
  47.8 0.6 copy-start.22
  48.4 12.4 %copy-start.24 = (f32[64,128]{1,0:T(8,128)}, f32[64,128]{1,0:T(8,128)S(1)}, u32[]{:S(2)}) copy-start(f32[64,128]{1,0:T(8,128)S(1)} %get-tuple-element.87.refs_11_) | copy-start | bytes 98308
  48.4 14.3 %collective-permute-start.13 = (f32[1056,128]{1,0:T(8,128)S(1)}, f32[1056,128]{1,0:T(8,128)S(1)}, u32[]{:S(2)}, u32[]{:S(2)}) collective-permute-start(f32[1056,128]{1,0:T(8,128)S(1)} %get-tuple-element.76.refs_0_), channel_id=1, source_target_pairs={{0,3},{1,0},{2,1},{3,2},{4,7},{5,4},{6,5},{7,6},{8,11},{9,8},{10,9... | collective-permute-start | bytes 1622024 | tf_op jit(solution)/shard_map/ppermute | solution.py:643
  49.9 16.0 %collective-permute-start.12 = (f32[1056,128]{1,0:T(8,128)S(1)}, f32[1056,128]{1,0:T(8,128)S(1)}, u32[]{:S(2)}, u32[]{:S(2)}) collective-permute-start(f32[1056,128]{1,0:T(8,128)S(1)} %get-tuple-element.76.refs_0_), channel_id=1, source_target_pairs={{0,1},{1,2},{2,3},{3,0},{4,5},{5,6},{6,7},{7,4},{8,9},{9,10},{10,1... | collective-permute-start | bytes 1622024 | tf_op jit(solution)/shard_map/ppermute | solution.py:643
  65.9 10.4 %collective-permute-start.14 = (f32[656,128]{1,0:T(8,128)S(1)}, f32[656,128]{1,0:T(8,128)}, u32[]{:S(2)}, u32[]{:S(2)}) collective-permute-start(f32[656,128]{1,0:T(8,128)S(1)} %slice.14), channel_id=1, source_target_pairs={{0,1},{1,2},{2,3},{3,0},{4,5},{5,6},{6,7},{7,4},{8,9},{9,10},{10,1... | collective-permute-start | bytes 1007624 | tf_op jit(solution)/shard_map/ppermute | solution.py:643
  66.2 7.1 %collective-permute-start.15 = (f32[400,128]{1,0:T(8,128)S(1)}, f32[400,128]{1,0:T(8,128)}, u32[]{:S(2)}, u32[]{:S(2)}) collective-permute-start(f32[400,128]{1,0:T(8,128)S(1)} %slice.15), channel_id=1, source_target_pairs={{0,3},{1,0},{2,1},{3,2},{4,7},{5,4},{6,5},{7,6},{8,11},{9,8},{10,9... | collective-permute-start | bytes 614408 | tf_op jit(solution)/shard_map/ppermute | solution.py:643
  69.3 10.9 %collective-permute-start.16 = (f32[1056,128]{1,0:T(8,128)S(1)}, f32[1056,128]{1,0:T(8,128)S(1)}, u32[]{:S(2)}, u32[]{:S(2)}) collective-permute-start(f32[1056,128]{1,0:T(8,128)S(1)} %get-tuple-element.76.refs_0_), channel_id=1, source_target_pairs={{0,4},{4,0},{8,12},{12,8},{16,20},{20,16},{24,28},{28,24},{32,36},... | collective-permute-start | bytes 1622024 | tf_op jit(solution)/shard_map/ppermute | solution.py:638
  69.3 19.7 %collective-permute-start.17 = (f32[1056,128]{1,0:T(8,128)S(1)}, f32[1056,128]{1,0:T(8,128)S(1)}, u32[]{:S(2)}, u32[]{:S(2)}) collective-permute-start(f32[1056,128]{1,0:T(8,128)S(1)} %collective-permute-done.12.refs_1_), channel_id=1, source_target_pairs={{0,4},{4,0},{8,12},{12,8},{16,20},{20,16},{24,28},{28,24},{32,36},... | collective-permute-start | bytes 1622024 | tf_op jit(solution)/shard_map/ppermute | solution.py:638
  69.8 19.2 %collective-permute-start.18 = (f32[1056,128]{1,0:T(8,128)S(1)}, f32[1056,128]{1,0:T(8,128)S(1)}, u32[]{:S(2)}, u32[]{:S(2)}) collective-permute-start(f32[1056,128]{1,0:T(8,128)S(1)} %collective-permute-done.13.refs_2_), channel_id=1, source_target_pairs={{0,4},{4,0},{8,12},{12,8},{16,20},{20,16},{24,28},{28,24},{32,36},... | collective-permute-start | bytes 1622024 | tf_op jit(solution)/shard_map/ppermute | solution.py:638
  76.3 12.7 %collective-permute-start.19 = (f32[656,128]{1,0:T(8,128)}, f32[656,128]{1,0:T(8,128)}, u32[]{:S(2)}, u32[]{:S(2)}) collective-permute-start(f32[656,128]{1,0:T(8,128)} %collective-permute-done.14.refs_3_), channel_id=1, source_target_pairs={{0,4},{4,0},{8,12},{12,8},{16,20},{20,16},{24,28},{28,24},{32,36},... | collective-permute-start | bytes 1007624 | tf_op jit(solution)/shard_map/ppermute | solution.py:638
  76.3 12.7 %collective-permute-start.20 = (f32[400,128]{1,0:T(8,128)}, f32[400,128]{1,0:T(8,128)}, u32[]{:S(2)}, u32[]{:S(2)}) collective-permute-start(f32[400,128]{1,0:T(8,128)} %collective-permute-done.15.refs_4_), channel_id=1, source_target_pairs={{0,4},{4,0},{8,12},{12,8},{16,20},{20,16},{24,28},{28,24},{32,36},... | collective-permute-start | bytes 614408 | tf_op jit(solution)/shard_map/ppermute | solution.py:638
  76.8 12.1 %all-to-all-start.2 = ((f32[8,24,128]{2,1,0:T(8,128)}), f32[8,24,128]{2,1,0:T(8,128)S(1)}, u32[]{:S(2)}, u32[]{:S(2)}) async-start(f32[8,24,128]{2,1,0:T(8,128)} %bitcast.13), calls=%async_computation.2 | async-start | bytes 196608 | tf_op jit(solution)/shard_map/all_to_all | solution.py:661
  89.0 2.0 copy-start.25
  180.1 13.1 %copy-start.1 = (f32[656,128]{1,0:T(8,128)S(1)}, f32[656,128]{1,0:T(8,128)}, u32[]{:S(2)}) copy-start(f32[656,128]{1,0:T(8,128)} %copy-done) | copy-start | bytes 1007620
  180.1 13.1 %copy-start.3 = (f32[656,128]{1,0:T(8,128)S(1)}, f32[656,128]{1,0:T(8,128)}, u32[]{:S(2)}) copy-start(f32[656,128]{1,0:T(8,128)} %copy-done.2) | copy-start | bytes 1007620
  180.1 13.1 %copy-start.5 = (f32[656,128]{1,0:T(8,128)S(1)}, f32[656,128]{1,0:T(8,128)}, u32[]{:S(2)}) copy-start(f32[656,128]{1,0:T(8,128)} %copy-done.4) | copy-start | bytes 1007620
  180.2 13.1 %copy-start.7 = (f32[656,128]{1,0:T(8,128)S(1)}, f32[656,128]{1,0:T(8,128)}, u32[]{:S(2)}) copy-start(f32[656,128]{1,0:T(8,128)} %copy-done.6) | copy-start | bytes 1007620
  180.2 13.1 %copy-start.9 = (f32[656,128]{1,0:T(8,128)S(1)}, f32[656,128]{1,0:T(8,128)}, u32[]{:S(2)}) copy-start(f32[656,128]{1,0:T(8,128)} %copy-done.8) | copy-start | bytes 1007620
  180.2 13.1 %copy-start.11 = (f32[656,128]{1,0:T(8,128)S(1)}, f32[656,128]{1,0:T(8,128)}, u32[]{:S(2)}) copy-start(f32[656,128]{1,0:T(8,128)} %copy-done.10) | copy-start | bytes 1007620
  180.2 13.1 %copy-start.13 = (f32[392,128]{1,0:T(8,128)S(1)}, f32[392,128]{1,0:T(8,128)}, u32[]{:S(2)}) copy-start(f32[392,128]{1,0:T(8,128)} %copy-done.12) | copy-start | bytes 602116
  180.2 13.1 %copy-start.15 = (f32[392,128]{1,0:T(8,128)S(1)}, f32[392,128]{1,0:T(8,128)}, u32[]{:S(2)}) copy-start(f32[392,128]{1,0:T(8,128)} %copy-done.14) | copy-start | bytes 602116
  180.2 13.1 %copy-start.21 = (f32[264,128]{1,0:T(8,128)S(1)}, f32[264,128]{1,0:T(8,128)}, u32[]{:S(2)}) copy-start(f32[264,128]{1,0:T(8,128)} %copy-done.20) | copy-start | bytes 405508
  181.6 11.8 %copy-start.19 = (f32[264,128]{1,0:T(8,128)S(1)}, f32[264,128]{1,0:T(8,128)}, u32[]{:S(2)}) copy-start(f32[264,128]{1,0:T(8,128)} %copy-done.18) | copy-start | bytes 405508
  193.8 12.6 %copy-start.23 = (f32[64,4,128]{2,1,0:T(4,128)S(1)}, f32[64,4,128]{2,1,0:T(4,128)}, u32[]{:S(2)}) copy-start(f32[64,4,128]{2,1,0:T(4,128)} %copy-done.22) | copy-start | bytes 393220
  206.4 11.6 %copy-start.17 = (f32[768,128]{1,0:T(8,128)S(1)}, f32[768,128]{1,0:T(8,128)}, u32[]{:S(2)}) copy-start(f32[768,128]{1,0:T(8,128)} %copy-done.16) | copy-start | bytes 1179652
  207.7 10.3 %copy-start.29 = (f32[8,128]{1,0:T(8,128)S(1)}, f32[8,128]{1,0:T(8,128)}, u32[]{:S(2)}) copy-start(f32[8,128]{1,0:T(8,128)} %copy-done.28) | copy-start | bytes 12292
  217.9 9.0 %copy-start.27 = (f32[8,128]{1,0:T(8,128)S(1)}, f32[8,128]{1,0:T(8,128)}, u32[]{:S(2)}) copy-start(f32[8,128]{1,0:T(8,128)} %copy-done.26) | copy-start | bytes 12292
  218.3 5.0 %collective-permute-start.23 = (f32[16,128]{1,0:T(8,128)S(1)}, f32[16,128]{1,0:T(8,128)S(1)}, u32[]{:S(2)}, u32[]{:S(2)}) collective-permute-start(f32[16,128]{1,0:T(8,128)S(1)} %shard_map.324.s0), channel_id=1, source_target_pairs={{0,3},{1,2},{2,1},{3,0},{4,7},{5,6},{6,5},{7,4},{8,11},{9,10},{10,... | collective-permute-start | bytes 24584 | tf_op jit(solution)/shard_map/ppermute | solution.py:638
  218.3 6.6 %collective-permute-start.22 = (f32[16,128]{1,0:T(8,128)S(1)}, f32[16,128]{1,0:T(8,128)S(1)}, u32[]{:S(2)}, u32[]{:S(2)}) collective-permute-start(f32[16,128]{1,0:T(8,128)S(1)} %shard_map.324.s0), channel_id=1, source_target_pairs={{0,2},{1,3},{2,0},{3,1},{4,6},{5,7},{6,4},{7,5},{8,10},{9,11},{10,... | collective-permute-start | bytes 24584 | tf_op jit(solution)/shard_map/ppermute | solution.py:638
  223.3 3.7 %collective-permute-start.21 = (f32[16,128]{1,0:T(8,128)S(1)}, f32[16,128]{1,0:T(8,128)S(1)}, u32[]{:S(2)}, u32[]{:S(2)}) collective-permute-start(f32[16,128]{1,0:T(8,128)S(1)} %shard_map.324.s0), channel_id=1, source_target_pairs={{0,1},{1,0},{2,3},{3,2},{4,5},{5,4},{6,7},{7,6},{8,9},{9,8},{10,11... | collective-permute-start | bytes 24584 | tf_op jit(solution)/shard_map/ppermute | solution.py:638
where the time goes:
time: 229 us; the launch traced here: 228 us
  blocking collectives  150 us (66%)
  waiting for transfers between devices  30.2 us (13%)
  starting transfers between devices  23.8 us (10%)
  Pallas kernels  20.8 us (9%)
  local copies, waits for them, and re-layouts  2.32 us (1%)
    all_to_all x10, blocking collectives, between(): lax.all_to_all(value, 'leaf', split_axis=0, concat_axis=0, tiled=True, ax...  128 us
    all_to_all x1, blocking collectives, route_leaf(): lax.all_to_all(value, ('leaf', 'grid'), split_axis=0, concat_axis=0, tile...  21.9 us
    pallas_call x17, Pallas kernels, run(): pl.pallas_call(kernel, out_shape=outs[0] if len(outs) == 1 else outs, scr...  20.8 us
    ppermute x8, waiting for transfers between devices, shift(): lax.ppermute(value, 'grid', [(s, (s + step) % size) for s in range(size)])  13.4 us
    ppermute x16, starting transfers between devices, swap(): return lax.ppermute(value, axis, pairs)  11 us
    ppermute x8, starting transfers between devices, shift(): lax.ppermute(value, 'grid', [(s, (s + step) % size) for s in range(size)])  9.53 us
    all_to_all x1, waiting for transfers between devices, between(): lax.all_to_all(value, 'leaf', split_axis=0, concat_axis=0, tiled=True, ax...  8.77 us
    ppermute x16, waiting for transfers between devices, swap(): return lax.ppermute(value, axis, pairs)  7.99 us
  transfers between devices with their start and end apart: 25, of which 12 were waited for; matrix products, arithmetic and copies ran while one was open for 0% of the time, Pallas kernels for 2%

commit v1 on v0

--- a/solution.py
+++ b/solution.py
@@ -714,21 +714,20 @@
         *sums, y_l, plan, rows, hold,
     )
     got_m = route_leaf(out)
-    m_prev, m_next = after(got_m, m_prev, m_next)
+    m_prev, m_next, pack_u = after(got_m, m_prev, m_next, pack_u)
     m_low, m_high = shift(m_prev[:MISC], 1), shift(m_next[MISC:], -1)
     m_prev_core, m_next_core = swap(m_prev, "leaf", 1), swap(m_next, "leaf", 1)
+    u_prev, u_next = shift(pack_u, 1), shift(pack_u, -1)
+    m_low_core, m_high_core = swap(m_low, "leaf", 1), swap(m_high, "leaf", 1)
     held_m = (
         pack_m, m_prev, m_next, m_low, m_high,
-        m_core, m_prev_core, m_next_core, swap(m_low, "leaf", 1), swap(m_high, "leaf", 1),
+        m_core, m_prev_core, m_next_core, m_low_core, m_high_core,
     )
 
     part, y_m, upd_m = run(
         enter_middle_kernel, [(8 * RHS, TILE), flat, high], *held_m, got_m,
         copied=VAT - SRC,
     )
-    (pack_u,) = after(part, pack_u)
-    u_prev = shift(pack_u, 1)
-    u_next = shift(pack_u, -1)
     red = between(part, 8)
     u_prev, u_next = after(red, u_prev, u_next)
     u_low, u_high = shift(u_prev[:END], 1), shift(u_next[END:], -1)

time: 229 us -> 233 us (1.017)
  blocking collectives: 150 us -> 128 us
  waiting for transfers between devices: 30.2 us -> 42.8 us
  starting transfers between devices: 23.8 us -> 36.3 us
    all_to_all x1 -> x0, blocking collectives: 21.9 us -> none  [route_leaf(): lax.all_to_all(value, ('leaf', 'grid'), split_axis=0, concat_axis=0, tile...]
    all_to_all x0 -> x1, starting transfers between devices: none -> 11.7 us  [route_leaf(): lax.all_to_all(value, ('leaf', 'grid'), split_axis=0, concat_axis=0, tile...]
    all_to_all x0 -> x1, waiting for transfers between devices: none -> 10.2 us  [route_leaf(): lax.all_to_all(value, ('leaf', 'grid'), split_axis=0, concat_axis=0, tile...]
  transfers between devices with their start and end apart: 25 -> 26, of which waited for: 12 -> 10; matrix products, arithmetic and copies ran while one was open for 0% -> 0% of each run, Pallas kernels for 2% -> 3%
where the time goes in v1:
time: 233 us
  blocking collectives  128 us (55%)
  waiting for transfers between devices  42.8 us (18%)
  starting transfers between devices  36.3 us (16%)
  Pallas kernels  21.5 us (9%)
  local copies, waits for them, and re-layouts  2.69 us (1%)
    all_to_all x10, blocking collectives, between(): lax.all_to_all(value, 'leaf', split_axis=0, concat_axis=0, tiled=True, ax...  128 us
    pallas_call x17, Pallas kernels, run(): pl.pallas_call(kernel, out_shape=outs[0] if len(outs) == 1 else outs, scr...  21.5 us
    ppermute x8, waiting for transfers between devices, shift(): lax.ppermute(value, 'grid', [(s, (s + step) % size) for s in range(size)])  14.6 us
    ppermute x16, starting transfers between devices, swap(): return lax.ppermute(value, axis, pairs)  12 us
    all_to_all x1, starting transfers between devices, route_leaf(): lax.all_to_all(value, ('leaf', 'grid'), split_axis=0, concat_axis=0, tile...  11.7 us
    all_to_all x1, waiting for transfers between devices, route_leaf(): lax.all_to_all(value, ('leaf', 'grid'), split_axis=0, concat_axis=0, tile...  10.2 us
    ppermute x16, waiting for transfers between devices, swap(): return lax.ppermute(value, axis, pairs)  9.26 us
    ppermute x8, starting transfers between devices, shift(): lax.ppermute(value, 'grid', [(s, (s + step) % size) for s in range(size)])  9.25 us
  transfers between devices with their start and end apart: 26, of which 10 were waited for; matrix products, arithmetic and copies ran while one was open for 0% of the time, Pallas kernels for 3%

profile of v1, /device:TPU:2, one launch (start us, length us, event | category | flops | bytes accessed | tf_op | source)
XLA Modules:
  0.0 232.5 jit_solution(5800908106068855529)
XLA Ops:
  0.6 1.5 shard_map.309
  2.1 1.6 collective-permute-start.2
  3.7 2.8 %collective-permute-start.1 = (f32[144,128]{1,0:T(8,128)S(1)}, f32[144,128]{1,0:T(8,128)S(1)}, u32[]{:S(2)}, u32[]{:S(2)}) collective-permute-start(f32[144,128]{1,0:T(8,128)S(1)} %get-tuple-element.64.s0), channel_id=1, source_target_pairs={{0,2},{1,3},{2,0},{3,1},{4,6},{5,7},{6,4},{7,5},{8,10},{9,11},{10,... | collective-permute-start | bytes 221192 | tf_op jit(solution)/shard_map/ppermute | solution.py:638
  6.5 0.0 collective-permute-start
  6.5 1.3 shard_map.310
  7.9 2.0 collective-permute-done.1.s2
  9.8 1.0 collective-permute-done.s1
  10.9 0.8 collective-permute-start.4
  11.7 1.2 collective-permute-start.3
  12.9 1.2 shard_map.311
  14.1 0.6 copy-done.26
  14.7 0.6 copy-done.28
  15.3 11.7 %all-to-all-start = ((f32[64,4,128]{2,1,0:T(4,128)}), f32[64,4,128]{2,1,0:T(4,128)S(1)}, u32[]{:S(2)}, u32[]{:S(2)}) async-start(f32[64,4,128]{2,1,0:T(4,128)} %bitcast.9), calls=%async_computation | async-start | bytes 262144 | tf_op jit(solution)/shard_map/all_to_all | solution.py:669
  27.0 0.2 collective-permute-start.7
  27.2 10.2 %all-to-all-done = f32[64,4,128]{2,1,0:T(4,128)S(1)} async-done(((f32[64,4,128]{2,1,0:T(4,128)}), f32[64,4,128]{2,1,0:T(4,128)S(1)}, u32[]{:S(2)}, u32[]{:S(2)}) %all-to-all-start) | async-done | bytes 131104 | tf_op jit(solution)/shard_map/all_to_all | solution.py:669
  37.4 0.0 collective-permute-done.4.refs_2_
  37.4 0.8 collective-permute-start.5
  38.2 1.3 collective-permute-start.13
  39.5 0.7 collective-permute-start.12
  40.2 2.0 collective-permute-start.6
  42.3 0.1 collective-permute-start.8
  42.4 11.4 %collective-permute-done.6.refs_4_ = f32[264,128]{1,0:T(8,128)S(1)} collective-permute-done((f32[264,128]{1,0:T(8,128)S(1)}, f32[264,128]{1,0:T(8,128)S(1)}, u32[]{:S(2)}, u32[]{:S(2)}) %collective-permute-start.6) | collective-permute-done | bytes 135200 | tf_op jit(solution)/shard_map/ppermute | solution.py:643
  53.8 0.5 collective-permute-start.11
  54.3 1.3 collective-permute-done.11.refs_9_
  55.6 0.1 collective-permute-start.10
  55.8 1.3 collective-permute-done.10.refs_8_
  57.1 0.7 copy-done.14
  57.8 2.0 shard_map.312
  59.8 0.7 copy-done.22
  60.5 10.9 %all_to_all.132 = f32[8,8,128]{2,1,0:T(8,128)S(1)} all-to-all(f32[8,8,128]{2,1,0:T(8,128)S(1)} %bitcast.57), channel_id=1, replica_groups={{0,8,16,24,32,40,48,56},{4,12,20,28,36,44,52,60},{64,72,80,88,96,104,11..., dimensions={0} | all-to-all | bytes 65536 | tf_op jit(solution)/shard_map/all_to_all | solution.py:661
  71.4 2.0 collective-permute-start.14
  73.4 0.4 collective-permute-start.15
  73.8 0.5 collective-permute-start.17
  74.3 2.9 %shard_map.313 = (f32[192,128]{1,0:T(8,128)}, f32[8,1024]{1,0:T(8,128)S(1)}, f32[8,128]{1,0:T(8,128)S(1)}) custom-call(f32[656,128]{1,0:T(8,128)} %copy-done.4, f32[656,128]{1,0:T(8,128)} %copy-done, f32[656,128]{1,0:T(8,128)} %copy-done.2, f32[392,128]{1,0:T(8,128)} %copy-done.12, f32[264,128]{1,0:T(8,128)} %copy-done.18, f32[656,128]{1,0:T(8,128)} %copy-done.6, ...), custom_call_target="tpu_custom_call" | custom-call | tf_op jit(solution)/shard_map/pallas_call | solution.py:623
  77.2 3.1 %collective-permute-done.15.refs_4_ = f32[400,128]{1,0:T(8,128)} collective-permute-done((f32[400,128]{1,0:T(8,128)S(1)}, f32[400,128]{1,0:T(8,128)}, u32[]{:S(2)}, u32[]{:S(2)}) %collective-permute-start.15) | collective-permute-done | bytes 204832 | tf_op jit(solution)/shard_map/ppermute | solution.py:643
  80.3 0.0 collective-permute-done.14.refs_3_
  80.3 0.5 collective-permute-start.20
  80.8 3.4 %all-to-all-start.2 = ((f32[8,24,128]{2,1,0:T(8,128)}), f32[8,24,128]{2,1,0:T(8,128)S(1)}, u32[]{:S(2)}, u32[]{:S(2)}) async-start(f32[8,24,128]{2,1,0:T(8,128)} %bitcast.13), calls=%async_computation.2 | async-start | bytes 196608 | tf_op jit(solution)/shard_map/all_to_all | solution.py:661
  84.2 8.8 %all-to-all-done.2 = f32[8,24,128]{2,1,0:T(8,128)S(1)} async-done(((f32[8,24,128]{2,1,0:T(8,128)}), f32[8,24,128]{2,1,0:T(8,128)S(1)}, u32[]{:S(2)}, u32[]{:S(2)}) %all-to-all-start.2) | async-done | bytes 98336 | tf_op jit(solution)/shard_map/all_to_all | solution.py:661
  93.0 2.0 shard_map.314
  95.0 1.8 shard_map.315
  96.8 11.3 %all_to_all.133 = f32[16,16,128]{2,1,0:T(8,128)S(1)} all-to-all(f32[16,16,128]{2,1,0:T(8,128)S(1)} %bitcast.51), channel_id=1, replica_groups={{0,8,16,24,32,40,48,56,64,72,80,88,96,104,112,120},{4,12,20,28,36,44,52..., dimensions={0} | all-to-all | bytes 262144 | tf_op jit(solution)/shard_map/all_to_all | solution.py:661
  108.2 1.0 shard_map.316
  109.2 11.8 %all_to_all.134 = f32[16,24,128]{2,1,0:T(8,128)S(1)} all-to-all(f32[16,24,128]{2,1,0:T(8,128)S(1)} %bitcast.49), channel_id=1, replica_groups={{0,8,16,24,32,40,48,56,64,72,80,88,96,104,112,120},{4,12,20,28,36,44,52..., dimensions={0} | all-to-all | bytes 393216 | tf_op jit(solution)/shard_map/all_to_all | solution.py:661
  121.0 0.9 shard_map.317
  121.9 17.1 %all_to_all.135 = f32[32,16,128]{2,1,0:T(8,128)S(1)} all-to-all(f32[32,16,128]{2,1,0:T(8,128)S(1)} %bitcast.48), channel_id=1, replica_groups={{0,8,16,24,32,40,48,56,64,72,80,88,96,104,112,120,128,136,144,152,160,1..., dimensions={0} | all-to-all | bytes 524288 | tf_op jit(solution)/shard_map/all_to_all | solution.py:661
  138.9 0.8 shard_map.318
  139.7 15.9 %all_to_all.136 = f32[32,24,128]{2,1,0:T(8,128)S(1)} all-to-all(f32[32,24,128]{2,1,0:T(8,128)S(1)} %bitcast.46), channel_id=1, replica_groups={{0,8,16,24,32,40,48,56,64,72,80,88,96,104,112,120,128,136,144,152,160,1..., dimensions={0} | all-to-all | bytes 786432 | tf_op jit(solution)/shard_map/all_to_all | solution.py:661
  155.6 1.3 shard_map.319
  157.0 15.5 %all_to_all.137 = f32[32,8,128]{2,1,0:T(8,128)S(1)} all-to-all(f32[32,8,128]{2,1,0:T(8,128)S(1)} %bitcast.52), channel_id=1, replica_groups={{0,8,16,24,32,40,48,56,64,72,80,88,96,104,112,120,128,136,144,152,160,1..., dimensions={0} | all-to-all | bytes 262144 | tf_op jit(solution)/shard_map/all_to_all | solution.py:661
  172.5 0.4 shard_map.320
  172.9 11.2 %all_to_all.138 = f32[16,16,128]{2,1,0:T(8,128)S(1)} all-to-all(f32[16,16,128]{2,1,0:T(8,128)S(1)} %bitcast.54), channel_id=1, replica_groups={{0,8,16,24,32,40,48,56,64,72,80,88,96,104,112,120},{4,12,20,28,36,44,52..., dimensions={0} | all-to-all | bytes 262144 | tf_op jit(solution)/shard_map/all_to_all | solution.py:661
  184.2 1.4 shard_map.321
  185.5 11.7 %all_to_all.139 = f32[16,8,128]{2,1,0:T(8,128)S(1)} all-to-all(f32[16,8,128]{2,1,0:T(8,128)S(1)} %bitcast.55), channel_id=1, replica_groups={{0,8,16,24,32,40,48,56,64,72,80,88,96,104,112,120},{4,12,20,28,36,44,52..., dimensions={0} | all-to-all | bytes 131072 | tf_op jit(solution)/shard_map/all_to_all | solution.py:661
  197.3 0.4 shard_map.322
  197.7 12.6 %all_to_all.140 = f32[8,32,128]{2,1,0:T(8,128)S(1)} all-to-all(f32[8,32,128]{2,1,0:T(8,128)S(1)} %bitcast.53), channel_id=1, replica_groups={{0,8,16,24,32,40,48,56},{4,12,20,28,36,44,52,60},{64,72,80,88,96,104,11..., dimensions={0} | all-to-all | bytes 262144 | tf_op jit(solution)/shard_map/all_to_all | solution.py:661
  210.3 1.3 shard_map.323
  211.7 10.3 %all_to_all.141 = f32[8,4,128]{2,1,0:T(4,128)S(1)} all-to-all(f32[8,4,128]{2,1,0:T(4,128)S(1)} %bitcast.58), channel_id=1, replica_groups={{0,8,16,24,32,40,48,56},{4,12,20,28,36,44,52,60},{64,72,80,88,96,104,11..., dimensions={0} | all-to-all | bytes 32768 | tf_op jit(solution)/shard_map/all_to_all | solution.py:661
  221.9 0.3 shard_map.324.s0
  222.3 2.1 collective-permute-start.23
  224.4 3.5 %collective-permute-start.22 = (f32[16,128]{1,0:T(8,128)S(1)}, f32[16,128]{1,0:T(8,128)S(1)}, u32[]{:S(2)}, u32[]{:S(2)}) collective-permute-start(f32[16,128]{1,0:T(8,128)S(1)} %shard_map.324.s0), channel_id=1, source_target_pairs={{0,2},{1,3},{2,0},{3,1},{4,6},{5,7},{6,4},{7,5},{8,10},{9,11},{10,... | collective-permute-start | bytes 24584 | tf_op jit(solution)/shard_map/ppermute | solution.py:638
  227.9 1.6 collective-permute-done.22.s2
  229.6 2.0 collective-permute-done.21.s1
  231.6 0.9 shard_map.325
  (79 shorter events, 0.2 us)
Async XLA Ops:
  2.1 10.8 %copy-start.16 = (f32[768,128]{1,0:T(8,128)}, f32[768,128]{1,0:T(8,128)S(1)}, u32[]{:S(2)}) copy-start(f32[768,128]{1,0:T(8,128)S(1)} %get-tuple-element.71.hold) | copy-start | bytes 1179652
  2.1 5.8 %collective-permute-start.2 = (f32[144,128]{1,0:T(8,128)S(1)}, f32[144,128]{1,0:T(8,128)S(1)}, u32[]{:S(2)}, u32[]{:S(2)}) collective-permute-start(f32[144,128]{1,0:T(8,128)S(1)} %get-tuple-element.64.s0), channel_id=1, source_target_pairs={{0,3},{1,2},{2,1},{3,0},{4,7},{5,6},{6,5},{7,4},{8,11},{9,10},{10,... | collective-permute-start | bytes 221192 | tf_op jit(solution)/shard_map/ppermute | solution.py:638
  3.7 6.1 %collective-permute-start.1 = (f32[144,128]{1,0:T(8,128)S(1)}, f32[144,128]{1,0:T(8,128)S(1)}, u32[]{:S(2)}, u32[]{:S(2)}) collective-permute-start(f32[144,128]{1,0:T(8,128)S(1)} %get-tuple-element.64.s0), channel_id=1, source_target_pairs={{0,2},{1,3},{2,0},{3,1},{4,6},{5,7},{6,4},{7,5},{8,10},{9,11},{10,... | collective-permute-start | bytes 221192 | tf_op jit(solution)/shard_map/ppermute | solution.py:638
  6.5 4.4 %collective-permute-start = (f32[144,128]{1,0:T(8,128)S(1)}, f32[144,128]{1,0:T(8,128)S(1)}, u32[]{:S(2)}, u32[]{:S(2)}) collective-permute-start(f32[144,128]{1,0:T(8,128)S(1)} %get-tuple-element.64.s0), channel_id=1, source_target_pairs={{0,1},{1,0},{2,3},{3,2},{4,5},{5,4},{6,7},{7,6},{8,9},{9,8},{10,11... | collective-permute-start | bytes 221192 | tf_op jit(solution)/shard_map/ppermute | solution.py:638
  7.9 19.1 %copy-start.4 = (f32[656,128]{1,0:T(8,128)}, f32[656,128]{1,0:T(8,128)S(1)}, u32[]{:S(2)}) copy-start(f32[656,128]{1,0:T(8,128)S(1)} %get-tuple-element.62.refs_0_) | copy-start | bytes 1007620
  10.9 26.5 %collective-permute-start.4 = (f32[656,128]{1,0:T(8,128)S(1)}, f32[656,128]{1,0:T(8,128)S(1)}, u32[]{:S(2)}, u32[]{:S(2)}) collective-permute-start(f32[656,128]{1,0:T(8,128)S(1)} %get-tuple-element.62.refs_0_), channel_id=1, source_target_pairs={{0,3},{1,0},{2,1},{3,2},{4,7},{5,4},{6,5},{7,6},{8,11},{9,8},{10,9... | collective-permute-start | bytes 1007624 | tf_op jit(solution)/shard_map/ppermute | solution.py:643
  11.7 25.7 %collective-permute-start.3 = (f32[656,128]{1,0:T(8,128)S(1)}, f32[656,128]{1,0:T(8,128)S(1)}, u32[]{:S(2)}, u32[]{:S(2)}) collective-permute-start(f32[656,128]{1,0:T(8,128)S(1)} %get-tuple-element.62.refs_0_), channel_id=1, source_target_pairs={{0,1},{1,2},{2,3},{3,0},{4,5},{5,6},{6,7},{7,4},{8,9},{9,10},{10,1... | collective-permute-start | bytes 1007624 | tf_op jit(solution)/shard_map/ppermute | solution.py:643
  14.1 0.6 copy-start.26
  14.7 0.6 copy-start.28
  15.3 22.1 %all-to-all-start = ((f32[64,4,128]{2,1,0:T(4,128)}), f32[64,4,128]{2,1,0:T(4,128)S(1)}, u32[]{:S(2)}, u32[]{:S(2)}) async-start(f32[64,4,128]{2,1,0:T(4,128)} %bitcast.9), calls=%async_computation | async-start | bytes 262144 | tf_op jit(solution)/shard_map/all_to_all | solution.py:669
  27.0 15.3 %collective-permute-start.7 = (f32[656,128]{1,0:T(8,128)S(1)}, f32[656,128]{1,0:T(8,128)S(1)}, u32[]{:S(2)}, u32[]{:S(2)}) collective-permute-start(f32[656,128]{1,0:T(8,128)S(1)} %get-tuple-element.62.refs_0_), channel_id=1, source_target_pairs={{0,4},{4,0},{8,12},{12,8},{16,20},{20,16},{24,28},{28,24},{32,36},... | collective-permute-start | bytes 1007624 | tf_op jit(solution)/shard_map/ppermute | solution.py:638
  37.4 16.4 %copy-start.2 = (f32[656,128]{1,0:T(8,128)}, f32[656,128]{1,0:T(8,128)S(1)}, u32[]{:S(2)}) copy-start(f32[656,128]{1,0:T(8,128)S(1)} %collective-permute-done.4.refs_2_) | copy-start | bytes 1007620
  37.4 4.9 %copy-start = (f32[656,128]{1,0:T(8,128)}, f32[656,128]{1,0:T(8,128)S(1)}, u32[]{:S(2)}) copy-start(f32[656,128]{1,0:T(8,128)S(1)} %collective-permute-done.3.refs_1_) | copy-start | bytes 1007620
  37.4 16.4 %collective-permute-start.5 = (f32[392,128]{1,0:T(8,128)S(1)}, f32[392,128]{1,0:T(8,128)S(1)}, u32[]{:S(2)}, u32[]{:S(2)}) collective-permute-start(f32[392,128]{1,0:T(8,128)S(1)} %slice.12), channel_id=1, source_target_pairs={{0,1},{1,2},{2,3},{3,0},{4,5},{5,6},{6,7},{7,4},{8,9},{9,10},{10,1... | collective-permute-start | bytes 602120 | tf_op jit(solution)/shard_map/ppermute | solution.py:643
  38.2 33.1 %collective-permute-start.13 = (f32[1056,128]{1,0:T(8,128)S(1)}, f32[1056,128]{1,0:T(8,128)S(1)}, u32[]{:S(2)}, u32[]{:S(2)}) collective-permute-start(f32[1056,128]{1,0:T(8,128)S(1)} %get-tuple-element.75.refs_0_), channel_id=1, source_target_pairs={{0,3},{1,0},{2,1},{3,2},{4,7},{5,4},{6,5},{7,6},{8,11},{9,8},{10,9... | collective-permute-start | bytes 1622024 | tf_op jit(solution)/shard_map/ppermute | solution.py:643
  39.5 31.8 %collective-permute-start.12 = (f32[1056,128]{1,0:T(8,128)S(1)}, f32[1056,128]{1,0:T(8,128)S(1)}, u32[]{:S(2)}, u32[]{:S(2)}) collective-permute-start(f32[1056,128]{1,0:T(8,128)S(1)} %get-tuple-element.75.refs_0_), channel_id=1, source_target_pairs={{0,1},{1,2},{2,3},{3,0},{4,5},{5,6},{6,7},{7,4},{8,9},{9,10},{10,1... | collective-permute-start | bytes 1622024 | tf_op jit(solution)/shard_map/ppermute | solution.py:643
  40.2 13.6 %collective-permute-start.6 = (f32[264,128]{1,0:T(8,128)S(1)}, f32[264,128]{1,0:T(8,128)S(1)}, u32[]{:S(2)}, u32[]{:S(2)}) collective-permute-start(f32[264,128]{1,0:T(8,128)S(1)} %slice.13), channel_id=1, source_target_pairs={{0,3},{1,0},{2,1},{3,2},{4,7},{5,4},{6,5},{7,6},{8,11},{9,8},{10,9... | collective-permute-start | bytes 405512 | tf_op jit(solution)/shard_map/ppermute | solution.py:643
  42.3 14.8 %copy-start.6 = (f32[656,128]{1,0:T(8,128)}, f32[656,128]{1,0:T(8,128)S(1)}, u32[]{:S(2)}) copy-start(f32[656,128]{1,0:T(8,128)S(1)} %collective-permute-done.7.refs_5_) | copy-start | bytes 1007620
  42.3 13.5 %collective-permute-start.8 = (f32[656,128]{1,0:T(8,128)S(1)}, f32[656,128]{1,0:T(8,128)S(1)}, u32[]{:S(2)}, u32[]{:S(2)}) collective-permute-start(f32[656,128]{1,0:T(8,128)S(1)} %collective-permute-done.3.refs_1_), channel_id=1, source_target_pairs={{0,4},{4,0},{8,12},{12,8},{16,20},{20,16},{24,28},{28,24},{32,36},... | collective-permute-start | bytes 1007624 | tf_op jit(solution)/shard_map/ppermute | solution.py:638
  53.8 3.3 %copy-start.18 = (f32[264,128]{1,0:T(8,128)}, f32[264,128]{1,0:T(8,128)S(1)}, u32[]{:S(2)}) copy-start(f32[264,128]{1,0:T(8,128)S(1)} %collective-permute-done.6.refs_4_) | copy-start | bytes 405508
  53.8 2.0 collective-permute-start.9
  53.8 3.3 %copy-start.12 = (f32[392,128]{1,0:T(8,128)}, f32[392,128]{1,0:T(8,128)S(1)}, u32[]{:S(2)}) copy-start(f32[392,128]{1,0:T(8,128)S(1)} %collective-permute-done.5.refs_3_) | copy-start | bytes 602116
  53.8 1.8 collective-permute-start.11
  55.6 1.5 copy-start.20
  55.6 1.4 collective-permute-start.10
  55.8 1.3 copy-start.8
  55.8 1.3 copy-start.10
  57.1 0.7 copy-start.14
  59.8 0.7 copy-start.22
  60.5 10.9 %copy-start.24 = (f32[64,128]{1,0:T(8,128)}, f32[64,128]{1,0:T(8,128)S(1)}, u32[]{:S(2)}) copy-start(f32[64,128]{1,0:T(8,128)S(1)} %get-tuple-element.87.refs_11_) | copy-start | bytes 98308
  71.4 8.9 %collective-permute-start.14 = (f32[656,128]{1,0:T(8,128)S(1)}, f32[656,128]{1,0:T(8,128)}, u32[]{:S(2)}, u32[]{:S(2)}) collective-permute-start(f32[656,128]{1,0:T(8,128)S(1)} %slice.14), channel_id=1, source_target_pairs={{0,1},{1,2},{2,3},{3,0},{4,5},{5,6},{6,7},{7,4},{8,9},{9,10},{10,1... | collective-permute-start | bytes 1007624 | tf_op jit(solution)/shard_map/ppermute | solution.py:643
  73.4 6.9 %collective-permute-start.15 = (f32[400,128]{1,0:T(8,128)S(1)}, f32[400,128]{1,0:T(8,128)}, u32[]{:S(2)}, u32[]{:S(2)}) collective-permute-start(f32[400,128]{1,0:T(8,128)S(1)} %slice.15), channel_id=1, source_target_pairs={{0,3},{1,0},{2,1},{3,2},{4,7},{5,4},{6,5},{7,6},{8,11},{9,8},{10,9... | collective-permute-start | bytes 614408 | tf_op jit(solution)/shard_map/ppermute | solution.py:643
  73.8 10.4 %collective-permute-start.16 = (f32[1056,128]{1,0:T(8,128)S(1)}, f32[1056,128]{1,0:T(8,128)S(1)}, u32[]{:S(2)}, u32[]{:S(2)}) collective-permute-start(f32[1056,128]{1,0:T(8,128)S(1)} %get-tuple-element.75.refs_0_), channel_id=1, source_target_pairs={{0,4},{4,0},{8,12},{12,8},{16,20},{20,16},{24,28},{28,24},{32,36},... | collective-permute-start | bytes 1622024 | tf_op jit(solution)/shard_map/ppermute | solution.py:638
  73.8 19.2 %collective-permute-start.17 = (f32[1056,128]{1,0:T(8,128)S(1)}, f32[1056,128]{1,0:T(8,128)S(1)}, u32[]{:S(2)}, u32[]{:S(2)}) collective-permute-start(f32[1056,128]{1,0:T(8,128)S(1)} %collective-permute-done.12.refs_1_), channel_id=1, source_target_pairs={{0,4},{4,0},{8,12},{12,8},{16,20},{20,16},{24,28},{28,24},{32,36},... | collective-permute-start | bytes 1622024 | tf_op jit(solution)/shard_map/ppermute | solution.py:638
  74.3 18.7 %collective-permute-start.18 = (f32[1056,128]{1,0:T(8,128)S(1)}, f32[1056,128]{1,0:T(8,128)S(1)}, u32[]{:S(2)}, u32[]{:S(2)}) collective-permute-start(f32[1056,128]{1,0:T(8,128)S(1)} %collective-permute-done.13.refs_2_), channel_id=1, source_target_pairs={{0,4},{4,0},{8,12},{12,8},{16,20},{20,16},{24,28},{28,24},{32,36},... | collective-permute-start | bytes 1622024 | tf_op jit(solution)/shard_map/ppermute | solution.py:638
  80.3 12.7 %collective-permute-start.19 = (f32[656,128]{1,0:T(8,128)}, f32[656,128]{1,0:T(8,128)}, u32[]{:S(2)}, u32[]{:S(2)}) collective-permute-start(f32[656,128]{1,0:T(8,128)} %collective-permute-done.14.refs_3_), channel_id=1, source_target_pairs={{0,4},{4,0},{8,12},{12,8},{16,20},{20,16},{24,28},{28,24},{32,36},... | collective-permute-start | bytes 1007624 | tf_op jit(solution)/shard_map/ppermute | solution.py:638
  80.3 12.7 %collective-permute-start.20 = (f32[400,128]{1,0:T(8,128)}, f32[400,128]{1,0:T(8,128)}, u32[]{:S(2)}, u32[]{:S(2)}) collective-permute-start(f32[400,128]{1,0:T(8,128)} %collective-permute-done.15.refs_4_), channel_id=1, source_target_pairs={{0,4},{4,0},{8,12},{12,8},{16,20},{20,16},{24,28},{28,24},{32,36},... | collective-permute-start | bytes 614408 | tf_op jit(solution)/shard_map/ppermute | solution.py:638
  80.8 12.1 %all-to-all-start.2 = ((f32[8,24,128]{2,1,0:T(8,128)}), f32[8,24,128]{2,1,0:T(8,128)S(1)}, u32[]{:S(2)}, u32[]{:S(2)}) async-start(f32[8,24,128]{2,1,0:T(8,128)} %bitcast.13), calls=%async_computation.2 | async-start | bytes 196608 | tf_op jit(solution)/shard_map/all_to_all | solution.py:661
  93.0 2.0 copy-start.25
  184.1 13.1 %copy-start.1 = (f32[656,128]{1,0:T(8,128)S(1)}, f32[656,128]{1,0:T(8,128)}, u32[]{:S(2)}) copy-start(f32[656,128]{1,0:T(8,128)} %copy-done) | copy-start | bytes 1007620
  184.1 13.1 %copy-start.3 = (f32[656,128]{1,0:T(8,128)S(1)}, f32[656,128]{1,0:T(8,128)}, u32[]{:S(2)}) copy-start(f32[656,128]{1,0:T(8,128)} %copy-done.2) | copy-start | bytes 1007620
  184.1 13.1 %copy-start.5 = (f32[656,128]{1,0:T(8,128)S(1)}, f32[656,128]{1,0:T(8,128)}, u32[]{:S(2)}) copy-start(f32[656,128]{1,0:T(8,128)} %copy-done.4) | copy-start | bytes 1007620
  184.1 13.1 %copy-start.7 = (f32[656,128]{1,0:T(8,128)S(1)}, f32[656,128]{1,0:T(8,128)}, u32[]{:S(2)}) copy-start(f32[656,128]{1,0:T(8,128)} %copy-done.6) | copy-start | bytes 1007620
  184.1 13.1 %copy-start.9 = (f32[656,128]{1,0:T(8,128)S(1)}, f32[656,128]{1,0:T(8,128)}, u32[]{:S(2)}) copy-start(f32[656,128]{1,0:T(8,128)} %copy-done.8) | copy-start | bytes 1007620
  184.1 13.1 %copy-start.11 = (f32[656,128]{1,0:T(8,128)S(1)}, f32[656,128]{1,0:T(8,128)}, u32[]{:S(2)}) copy-start(f32[656,128]{1,0:T(8,128)} %copy-done.10) | copy-start | bytes 1007620
  184.2 13.1 %copy-start.13 = (f32[392,128]{1,0:T(8,128)S(1)}, f32[392,128]{1,0:T(8,128)}, u32[]{:S(2)}) copy-start(f32[392,128]{1,0:T(8,128)} %copy-done.12) | copy-start | bytes 602116
  184.2 13.1 %copy-start.15 = (f32[392,128]{1,0:T(8,128)S(1)}, f32[392,128]{1,0:T(8,128)}, u32[]{:S(2)}) copy-start(f32[392,128]{1,0:T(8,128)} %copy-done.14) | copy-start | bytes 602116
  184.2 13.1 %copy-start.21 = (f32[264,128]{1,0:T(8,128)S(1)}, f32[264,128]{1,0:T(8,128)}, u32[]{:S(2)}) copy-start(f32[264,128]{1,0:T(8,128)} %copy-done.20) | copy-start | bytes 405508
  185.5 11.8 %copy-start.19 = (f32[264,128]{1,0:T(8,128)S(1)}, f32[264,128]{1,0:T(8,128)}, u32[]{:S(2)}) copy-start(f32[264,128]{1,0:T(8,128)} %copy-done.18) | copy-start | bytes 405508
  197.7 12.6 %copy-start.23 = (f32[64,4,128]{2,1,0:T(4,128)S(1)}, f32[64,4,128]{2,1,0:T(4,128)}, u32[]{:S(2)}) copy-start(f32[64,4,128]{2,1,0:T(4,128)} %copy-done.22) | copy-start | bytes 393220
  210.3 11.6 %copy-start.17 = (f32[768,128]{1,0:T(8,128)S(1)}, f32[768,128]{1,0:T(8,128)}, u32[]{:S(2)}) copy-start(f32[768,128]{1,0:T(8,128)} %copy-done.16) | copy-start | bytes 1179652
  211.7 10.3 %copy-start.29 = (f32[8,128]{1,0:T(8,128)S(1)}, f32[8,128]{1,0:T(8,128)}, u32[]{:S(2)}) copy-start(f32[8,128]{1,0:T(8,128)} %copy-done.28) | copy-start | bytes 12292
  221.9 9.7 %copy-start.27 = (f32[8,128]{1,0:T(8,128)S(1)}, f32[8,128]{1,0:T(8,128)}, u32[]{:S(2)}) copy-start(f32[8,128]{1,0:T(8,128)} %copy-done.26) | copy-start | bytes 12292
  222.3 5.7 %collective-permute-start.23 = (f32[16,128]{1,0:T(8,128)S(1)}, f32[16,128]{1,0:T(8,128)S(1)}, u32[]{:S(2)}, u32[]{:S(2)}) collective-permute-start(f32[16,128]{1,0:T(8,128)S(1)} %shard_map.324.s0), channel_id=1, source_target_pairs={{0,3},{1,2},{2,1},{3,0},{4,7},{5,6},{6,5},{7,4},{8,11},{9,10},{10,... | collective-permute-start | bytes 24584 | tf_op jit(solution)/shard_map/ppermute | solution.py:638
  224.4 5.2 %collective-permute-start.22 = (f32[16,128]{1,0:T(8,128)S(1)}, f32[16,128]{1,0:T(8,128)S(1)}, u32[]{:S(2)}, u32[]{:S(2)}) collective-permute-start(f32[16,128]{1,0:T(8,128)S(1)} %shard_map.324.s0), channel_id=1, source_target_pairs={{0,2},{1,3},{2,0},{3,1},{4,6},{5,7},{6,4},{7,5},{8,10},{9,11},{10,... | collective-permute-start | bytes 24584 | tf_op jit(solution)/shard_map/ppermute | solution.py:638
  227.9 3.7 %collective-permute-start.21 = (f32[16,128]{1,0:T(8,128)S(1)}, f32[16,128]{1,0:T(8,128)S(1)}, u32[]{:S(2)}, u32[]{:S(2)}) collective-permute-start(f32[16,128]{1,0:T(8,128)S(1)} %shard_map.324.s0), channel_id=1, source_target_pairs={{0,1},{1,0},{2,3},{3,2},{4,5},{5,4},{6,7},{7,6},{8,9},{9,8},{10,11... | collective-permute-start | bytes 24584 | tf_op jit(solution)/shard_map/ppermute | solution.py:638
